TPU v7x, 128 devices: a whole 4x4x4 slice. The times are simulated.
128 devices in a mesh: section: 8 (over x, core), ep: 16 (over y, z).
Axes of the slice: x: 4, y: 4, z: 4, core: 2. Of those that a mesh axis runs over, the one named last changes fastest.
Arguments:
- output_grad: bfloat16 [8, 4096, 1024], P('section', 'ep'), may hold values from -6 to 6
- layer_input: bfloat16 [8, 4096, 1024], P('section', 'ep'), may hold values from -6 to 6
- expert_ids: int32 [8, 4096, 8], P('section', 'ep'), may hold values from 0 to 63, all different within a row; in each aligned block of 256 rows (0 to 255, 256 to 511, ..., all dimensions but the last counted through in order) at most 40 rows name the same one
- route_probs: bfloat16 [8, 4096, 8], P('section', 'ep'), may hold values from 0.049804688 to 0.44921875
- gate_weight: bfloat16 [8, 64, 1024, 384], P('section', 'ep'), may hold values from -0.1875 to 0.1875
- up_weight: bfloat16 [8, 64, 1024, 384], P('section', 'ep'), may hold values from -0.1875 to 0.1875
- down_weight: bfloat16 [8, 64, 384, 1024], P('section', 'ep'), may hold values from -0.3125 to 0.3125
- saved_inputs: bfloat16 [8, 64, 640, 1024], P('section', 'ep'), may hold values from -6 to 6
- saved_gate_grad: bfloat16 [8, 64, 640, 384], P('section', 'ep'), may hold values from -0.5 to 0.5
- saved_up_grad: bfloat16 [8, 64, 640, 384], P('section', 'ep'), may hold values from -0.5 to 0.5
- saved_counts: int32 [8, 64, 16], P('section', 'ep'), may hold values from 0 to 40, as said below
Outputs:
- upstream_grad: bfloat16 [8, 4096, 1024], P('section', 'ep')
- prob_grad: bfloat16 [8, 4096, 8], P('section', 'ep')
- gate_weight_grad: bfloat16 [8, 64, 1024, 384], P('section', 'ep')
- up_weight_grad: bfloat16 [8, 64, 1024, 384], P('section', 'ep')
Inputs may be any that keep to these rules, and one draw needn't show every extreme that they name: `expert_ids`: each token names 8 different experts. Among the tokens of one device (aligned blocks of 256 tokens of a section) no expert is named more than 40 times, a bound that some block reaches. `saved_counts`: rows of a block at or beyond its count are padding; some block is full in every draw.
All inputs are finite; a program needn't handle non-finite values.
Results may differ from a plain program's by a relative error of at most 0.008.
Values may be sent and summed in bfloat16 or wider, within the bound.
No kernel may reach another device: no remote copies, remote signals or barrier semaphores. Data moves between devices by JAX's collectives and lax.ppermute only.
A program may use at most 128 MiB of HBM per device.

v0:
```python
import functools

import jax
import jax.numpy as jnp
from jax import lax
from jax.experimental import pallas as pl
from jax.experimental.pallas import tpu as pltpu
from jax.sharding import PartitionSpec as P


BF = jnp.bfloat16
F32 = jnp.float32
SIDE = 4
CAP = 40


def along_z(k):
    return [(4 * y + z, 4 * y + (z + k) % 4) for y in range(4) for z in range(4)]


def along_y(k):
    return [(4 * y + z, 4 * ((y + k) % 4) + z) for y in range(4) for z in range(4)]


def moved(array, pairs):
    return lax.ppermute(array, "ep", pairs)


def iota(shape, dim):
    return lax.broadcasted_iota(jnp.int32, shape, dim)


def expert_of_row(dest_ref, rows, per_dest, first, base):
    row = iota((rows, 256), 0)
    expert = jnp.zeros((rows, 256), jnp.int32)
    for i in range(SIDE):
        expert = jnp.where(row // per_dest == i, 4 * dest_ref[base + i] + first + row % per_dest, expert)
    return expert.astype(F32)


def earlier():
    return (iota((256, 256), 0) < iota((256, 256), 1)).astype(BF)


def slot_ranks(ids_list, expert, rows):
    marks = []
    for ids in ids_list:
        mark = jnp.zeros((rows, 256), F32)
        for k in range(8):
            mark = mark + jnp.where(ids[k : k + 1, :] == expert, 1.0, 0.0)
        marks.append(mark)
    mark = jnp.concatenate(marks, axis=0)
    rank = jnp.dot(mark.astype(BF), earlier(), preferred_element_type=F32)
    rank = jnp.where(mark > 0.0, rank, -1.0)
    return [rank[rows * j : rows * j + rows] for j in range(len(ids_list))]


def select_body(dest_ref, *refs, first):
    blocks, outs = refs[:8], refs[8:16]
    held, stage, in_sems, out_sems = refs[16:]
    order = [4 * c + j for j in range(4) for c in range(2)]
    loads = [pltpu.make_async_copy(blocks[n], held.at[n], in_sems.at[n]) for n in range(8)]
    for n in order:
        loads[n].start()
    experts = [expert_of_row(dest_ref, 8, 2, first, 4 * c) for c in range(2)]
    slot = iota((8, CAP, 256), 1).astype(F32)
    stores = []
    for n in order:
        loads[n].wait()
        c, j = n // 4, n % 4
        mine = slot_ranks([held[n, 256:264, 0:256].astype(F32)], experts[c], 8)[0]
        pick = jnp.where(mine[:, None, :] == slot, 1.0, 0.0).reshape(8 * CAP, 256).astype(BF)
        rows = jnp.dot(pick, held[n, 0:256, :], preferred_element_type=F32)
        for i in range(SIDE):
            for e in range(2):
                at = (2 * i + e) * CAP
                stage[n, i, e] = rows[at : at + CAP].astype(BF)
            store = pltpu.make_async_copy(stage.at[n, i], outs[4 * c + i].at[:, j], out_sems.at[4 * n + i])
            store.start()
            stores.append(store)
    for store in stores:
        store.wait()


def select(dest, blocks_a, blocks_b, first):
    out = jax.ShapeDtypeStruct((2, SIDE, CAP, 1024), BF)
    anywhere = pl.BlockSpec(memory_space=pl.ANY)
    outs = pl.pallas_call(
        functools.partial(select_body, first=first),
        out_shape=(out,) * 8,
        grid_spec=pltpu.PrefetchScalarGridSpec(
            num_scalar_prefetch=1,
            grid=(1,),
            in_specs=[anywhere] * 8,
            out_specs=[anywhere] * 8,
            scratch_shapes=[
                pltpu.VMEM((8, 264, 1024), BF),
                pltpu.VMEM((8, SIDE, 2, CAP, 1024), BF),
                pltpu.SemaphoreType.DMA((8,)),
                pltpu.SemaphoreType.DMA((32,)),
            ],
        ),
        name="select",
    )(dest, *blocks_a, *blocks_b)
    return outs[:4], outs[4:]


def spread_body(dest_ref, *refs):
    metas, outs = refs[:8], refs[8:]
    slot = iota((16, CAP, 256), 1).astype(F32)
    for c in range(2):
        expert = expert_of_row(dest_ref, 16, 4, 0, 4 * c)
        mine = metas[4 * c : 4 * c + 4]
        ids_list = [m[:, 0:256].astype(F32) for m in mine]
        ranks = slot_ranks(ids_list, expert, 16)
        for j in range(4):
            weight = mine[j][:, 256:512].astype(F32)
            scale = jnp.zeros((16, 256), F32)
            for k in range(8):
                scale = scale + jnp.where(ids_list[j][k : k + 1, :] == expert, weight[k : k + 1, :], 0.0)
            spread = jnp.where(ranks[j][:, None, :] == slot, scale[:, None, :], 0.0).reshape(16 * CAP, 256)
            outs[c][j] = spread.T.astype(BF)


def spreads(dest, blocks_a, blocks_b):
    return pl.pallas_call(
        spread_body,
        out_shape=(jax.ShapeDtypeStruct((SIDE, 256, 16 * CAP), BF),) * 2,
        grid_spec=pltpu.PrefetchScalarGridSpec(
            num_scalar_prefetch=1,
            grid=(1,),
            in_specs=[pl.BlockSpec((8, 1024), lambda g, d: (32, 0))] * 8,
            out_specs=[pl.BlockSpec((SIDE, 256, 16 * CAP), lambda g, d: (0, 0, 0))] * 2,
        ),
        name="spreads",
    )(dest, *blocks_a, *blocks_b)


def expert_body(*refs):
    xs, gs = refs[0:4], refs[4:8]
    wg_ref, wu_ref, wd_ref = refs[8:11]
    a_outs, b_outs = refs[-8:-4], refs[-4:]
    rows = jnp.concatenate([r[0] for r in xs], axis=0)
    grads = jnp.concatenate([r[0] for r in gs], axis=0)
    wg, wu, wd = wg_ref[0], wu_ref[0], wd_ref[0]
    nt = (((1,), (1,)), ((), ()))
    gate = jnp.dot(rows, wg, preferred_element_type=F32)
    up = jnp.dot(rows, wu, preferred_element_type=F32)
    hg = lax.dot_general(grads, wd, nt, preferred_element_type=F32)
    hg = jnp.concatenate(
        [hg[(4 * j + i) * CAP : (4 * j + i + 1) * CAP] for i in range(4) for j in range(4)], axis=0
    )
    sigma = jax.nn.sigmoid(gate)
    active = gate * sigma
    hidden = (active * up).astype(BF).astype(F32)
    prob = jnp.sum(hidden * hg, axis=1, keepdims=True)
    gate_grad = (hg * up * sigma * (1.0 + gate * (1.0 - sigma))).astype(BF)
    up_grad = (hg * active).astype(BF)
    lane = iota((CAP, 128), 1)
    for i in range(4):
        mine = jnp.zeros((CAP, 128), F32)
        for j in range(4):
            at = (4 * i + j) * CAP
            mine = jnp.where(lane == j, prob[at : at + CAP], mine)
        for t in range(5):
            a_outs[i][0, 160 + 8 * (t // 4) : 168 + 8 * (t // 4), 128 * (t % 4) : 128 * (t % 4) + 128] = mine[
                8 * t : 8 * t + 8
            ].astype(BF)
    back = lax.dot_general(gate_grad, wg, nt, preferred_element_type=F32)
    back = back + lax.dot_general(up_grad, wu, nt, preferred_element_type=F32)
    for i in range(4):
        for j in range(4):
            at = (4 * i + j) * CAP
            a_outs[i][0, CAP * j : CAP * j + CAP, :] = back[at : at + CAP, 0:512].astype(BF)
            b_outs[j][0, i] = back[at : at + CAP, 512:1024].astype(BF)


def experts(xs, gs, w_gate, w_up, w_down, half):
    rows = pl.BlockSpec((1, 160, 1024), lambda e: (e, 0, 0))
    w_in = pl.BlockSpec((1, 1024, 384), lambda e: (2 * half + e, 0, 0))
    w_out = pl.BlockSpec((1, 384, 1024), lambda e: (2 * half + e, 0, 0))
    flat = [a.reshape(2, 160, 1024) for a in (*xs, *gs)]
    outs = pl.pallas_call(
        expert_body,
        out_shape=(jax.ShapeDtypeStruct((2, 176, 512), BF),) * 4 + (jax.ShapeDtypeStruct((2, SIDE, CAP, 512), BF),) * 4,
        grid=(2,),
        in_specs=[rows] * 8 + [w_in, w_in, w_out],
        out_specs=[pl.BlockSpec((1, 176, 512), lambda e: (e, 0, 0))] * 4
        + [pl.BlockSpec((1, SIDE, CAP, 512), lambda e: (e, 0, 0, 0))] * 4,
        compiler_params=pltpu.CompilerParams(vmem_limit_bytes=56 * 1024 * 1024),
        name="experts",
    )(*flat, w_gate, w_up, w_down)
    return outs[0:4], outs[4:8]


def combine_body(*refs):
    spreads_in, rows_in, outs = refs[0:2], refs[2:18], refs[18:26]
    weights, rows, stage, weight_sems, row_sems, out_sems = refs[26:]

    def loads(c, j):
        at = 4 * c + j
        yield pltpu.make_async_copy(spreads_in[c].at[j], weights.at[at], weight_sems.at[at])
        for n in range(8):
            source = rows_in[8 * c + n]
            part = source.at[:, CAP * j : CAP * j + CAP] if c == 0 else source.at[:, j]
            yield pltpu.make_async_copy(part, rows.at[at, n], row_sems.at[8 * at + n])

    order = [(c, j) for j in ORDER_LAST_OWN for c in range(2)]
    for c, j in order:
        for load in loads(c, j):
            load.start()
    stores = []
    for c, j in order:
        for load in loads(c, j):
            load.wait()
        at = 4 * c + j
        pieces = [rows[at, n, e].astype(F32) for n in range(8) for e in range(2)]
        joined = jnp.concatenate(pieces, axis=0).astype(BF)
        stage[at] = jnp.dot(weights[at], joined, preferred_element_type=F32).astype(BF)
        store = pltpu.make_async_copy(stage.at[at], outs[at], out_sems.at[at])
        store.start()
        stores.append(store)
    for store in stores:
        store.wait()


ORDER_LAST_OWN = (1, 3, 2, 0)


def combine(spread_a, spread_b, lows, highs):
    both = [pair[half][i] for pair in (lows, highs) for i in range(4) for half in range(2)]
    anywhere = pl.BlockSpec(memory_space=pl.ANY)
    outs = pl.pallas_call(
        combine_body,
        out_shape=(jax.ShapeDtypeStruct((256, 512), BF),) * 8,
        in_specs=[anywhere] * 18,
        out_specs=[anywhere] * 8,
        scratch_shapes=[
            pltpu.VMEM((8, 256, 16 * CAP), BF),
            pltpu.VMEM((8, 8, 2, CAP, 512), BF),
            pltpu.VMEM((8, 256, 512), BF),
            pltpu.SemaphoreType.DMA((8,)),
            pltpu.SemaphoreType.DMA((64,)),
            pltpu.SemaphoreType.DMA((8,)),
        ],
        name="combine",
    )(spread_a, spread_b, *both)
    return outs[0:4], outs[4:8]


def gather_probs_body(dest_ref, *refs):
    metas, low, high, outs = refs[0:4], refs[4:8], refs[8:12], refs[12:16]
    slot = iota((CAP, 256), 0).astype(F32)
    expert = expert_of_row(dest_ref, 16, 4, 0, 0)
    ranks = slot_ranks([m[:, 0:256].astype(F32) for m in metas], expert, 16)
    found = [[] for _ in range(4)]
    for i in range(4):
        for e in range(4):
            source = low[i] if e < 2 else high[i]
            for j in range(4):
                total = jnp.zeros((1, 256), F32)
                for t in range(5):
                    column = source[e % 2, 8 * (t // 4) : 8 * (t // 4) + 8, 128 * (t % 4) : 128 * (t % 4) + 128]
                    column = column.astype(F32)[:, j : j + 1]
                    hit = ranks[j][4 * i + e : 4 * i + e + 1] == slot[8 * t : 8 * t + 8]
                    total = total + jnp.sum(jnp.where(hit, column, 0.0), axis=0, keepdims=True)
                found[j].append(total)
    for j in range(4):
        outs[j][...] = jnp.concatenate(found[j], axis=0).astype(BF)


def gather_probs(dest, blocks, low, high):
    tail = pl.BlockSpec((2, 16, 512), lambda g, d: (0, 10, 0))
    return pl.pallas_call(
        gather_probs_body,
        out_shape=(jax.ShapeDtypeStruct((16, 256), BF),) * 4,
        grid_spec=pltpu.PrefetchScalarGridSpec(
            num_scalar_prefetch=1,
            grid=(1,),
            in_specs=[pl.BlockSpec((8, 1024), lambda g, d: (32, 0))] * 4 + [tail] * 8,
            out_specs=[pl.BlockSpec((16, 256), lambda g, d: (0, 0))] * 4,
        ),
        name="gather_probs",
    )(dest, *blocks, *low, *high)


def pick_probs_body(place_ref, meta, *refs):
    tables, prob_ref = refs[0:4], refs[4]
    ids = meta[:, 0:256].astype(F32)
    found = [jnp.zeros((16, 256), F32) for _ in range(8)]
    for j in range(4):
        expert = expert_of_row(place_ref, 16, 4, 0, 4 * j)
        values = tables[j][...].astype(F32)
        for k in range(8):
            found[k] = found[k] + jnp.where(ids[k : k + 1, :] == expert, values, 0.0)
    rows = [jnp.sum(f, axis=0, keepdims=True) for f in found]
    prob_ref[...] = jnp.concatenate(rows, axis=0).astype(BF)


def pick_probs(places, block, tables):
    return pl.pallas_call(
        pick_probs_body,
        out_shape=jax.ShapeDtypeStruct((8, 256), BF),
        grid_spec=pltpu.PrefetchScalarGridSpec(
            num_scalar_prefetch=1,
            grid=(1,),
            in_specs=[pl.BlockSpec((8, 1024), lambda g, d: (32, 0))]
            + [pl.BlockSpec((16, 256), lambda g, d: (0, 0))] * 4,
            out_specs=pl.BlockSpec((8, 256), lambda g, d: (0, 0)),
        ),
        name="pick_probs",
    )(places, block, *tables)


def finish_body(*refs):
    left, right, out_ref = refs[0:4], refs[4:8], refs[8]
    for at, parts in ((0, left), (512, right)):
        total = parts[0][...].astype(F32)
        for part in parts[1:]:
            total = total + part[...].astype(F32)
        out_ref[0, :, at : at + 512] = total.astype(BF)


def finish(left, right):
    return pl.pallas_call(
        finish_body, out_shape=jax.ShapeDtypeStruct((1, 256, 1024), BF), name="finish"
    )(*left, *right)


def weight_grad(masked, grads):
    return jnp.einsum("esd,esf->edf", masked, grads, preferred_element_type=F32).astype(BF)


ORDER = (1, 3, 2)


def spread_out(arrays, pairs_of, sign=1):
    out = {0: arrays[0]}
    for k in ORDER:
        out[k] = moved(arrays[k], pairs_of(sign * k))
    return [out[k] for k in range(4)]


def per_device(
    output_grad,
    layer_input,
    expert_ids,
    route_probs,
    gate_weight,
    up_weight,
    down_weight,
    saved_inputs,
    saved_gate_grad,
    saved_up_grad,
    saved_counts,
):
    here = lax.axis_index("ep").astype(jnp.int32)
    sections = lax.axis_size("section")
    y, z = here // 4, here % 4
    steps = jnp.arange(4, dtype=jnp.int32)
    column = 4 * ((y + steps) % 4) + z
    row = 4 * y + (z + steps) % 4
    dest = jnp.concatenate([column, row])
    places = (4 * ((y + steps) % 4)[None, :] + ((z + steps) % 4)[:, None]).reshape(16)
    w_gate, w_up, w_down = gate_weight[0], up_weight[0], down_weight[0]

    meta = jnp.concatenate(
        [expert_ids[0].T.astype(BF), route_probs[0].T, jnp.zeros((8, 512), BF)], axis=1
    )
    block_a = jnp.concatenate([layer_input[0], meta], axis=0)
    block_b = jnp.concatenate([output_grad[0], meta], axis=0)
    blocks_a = spread_out([block_a] * 4, along_z)
    blocks_b = spread_out([block_b] * 4, along_y)

    live = jnp.arange(CAP, dtype=jnp.int32)[None, None, :] < saved_counts[0][:, :, None]
    masked = saved_inputs[0] * live.reshape(saved_inputs.shape[1:3]).astype(BF)[:, :, None]
    gate_part = weight_grad(masked, saved_gate_grad[0])
    up_part = weight_grad(masked, saved_up_grad[0])

    lows, highs = [], []
    for half in range(2):
        sent_a, sent_b = select(dest, blocks_a, blocks_b, 2 * half)
        xs = spread_out(sent_a, along_y)
        gs = spread_out(sent_b, along_z)
        back_a, back_b = experts(xs, gs, w_gate, w_up, w_down, half)
        lows.append(spread_out(back_a, along_y, -1))
        highs.append(spread_out(back_b, along_z, -1))
    spread_a, spread_b = spreads(dest, blocks_a, blocks_b)
    made_a, made_b = combine(spread_a, spread_b, lows, highs)
    left = spread_out(made_a, along_z, -1)
    right = spread_out(made_b, along_y, -1)
    tables = gather_probs(dest, blocks_a, lows[0], lows[1])
    tables = spread_out(tables, along_z, -1)
    input_grad = finish(left, right)
    upstream = lax.ppermute(input_grad, "section", [(s, s - 1) for s in range(1, sections)])
    prob_rows = pick_probs(places, block_a, tables)
    return (upstream, prob_rows.T[None], gate_part[None], up_part[None])


def solution(mesh):
    rows = P("section", "ep", None)
    stacks = P("section", "ep", None, None)

    return jax.shard_map(
        per_device,
        mesh=mesh,
        in_specs=(rows, rows, rows, rows) + (stacks,) * 6 + (rows,),
        out_specs=(rows, rows, stacks, stacks),
        check_vma=False,
    )
```

profile of v0, /device:TPU:1, one launch (start us, length us, event | category | flops | bytes accessed | tf_op | source)
XLA Modules:
  0.0 230.9 jit_solution(9909440260614997877)
XLA Ops:
  5.4 3.3 %collective-permute-start.1 = (bf16[264,1024]{1,0:T(8,128)(2,1)S(1)}, bf16[264,1024]{1,0:T(8,128)(2,1)}, u32[]{:S(2)}, u32[]{:S(2)}) collective-permute-start(bf16[264,1024]{1,0:T(8,128)(2,1)S(1)} %get-tuple-element.97.refs_0_.meta), channel_id=1, source_target_pairs={{0,2},{1,3},{2,0},{3,1},{4,6},{5,7},{6,4},{7,5},{8,10},{9,11},{10,... | collective-permute-start | bytes 1622024 | tf_op jit(solution)/shard_map/ppermute | solution.py:26
  13.3 6.3 %collective-permute-done.refs_1_ = bf16[264,1024]{1,0:T(8,128)(2,1)S(1)} collective-permute-done((bf16[264,1024]{1,0:T(8,128)(2,1)S(1)}, bf16[264,1024]{1,0:T(8,128)(2,1)S(1)}, u32[]{:S(2)}, u32[]{:S(2)}) %collective-permute-start) | collective-permute-done | bytes 540704 | tf_op jit(solution)/shard_map/ppermute | solution.py:26
  23.7 8.4 %collective-permute-done.1.refs_2_ = bf16[264,1024]{1,0:T(8,128)(2,1)} collective-permute-done((bf16[264,1024]{1,0:T(8,128)(2,1)S(1)}, bf16[264,1024]{1,0:T(8,128)(2,1)}, u32[]{:S(2)}, u32[]{:S(2)}) %collective-permute-start.1) | collective-permute-done | bytes 540704 | tf_op jit(solution)/shard_map/ppermute | solution.py:26
  32.1 3.8 %collective-permute-done.4.refs_6_ = bf16[264,1024]{1,0:T(8,128)(2,1)} collective-permute-done((bf16[264,1024]{1,0:T(8,128)(2,1)S(1)}, bf16[264,1024]{1,0:T(8,128)(2,1)}, u32[]{:S(2)}, u32[]{:S(2)}) %collective-permute-start.4) | collective-permute-done | bytes 540704 | tf_op jit(solution)/shard_map/ppermute | solution.py:26
  36.0 6.5 %select.29 = (bf16[2,4,40,1024]{3,2,1,0:T(8,128)(2,1)}, bf16[2,4,40,1024]{3,2,1,0:T(8,128)(2,1)}, bf16[2,4,40,1024]{3,2,1,0:T(8,128)(2,1)}, bf16[2,4,40,1024]{3,...) custom-call(s32[8]{0:T(128)} %pad_add_fusion.dest_ref, ...), custom_call_target="tpu_custom_call" | custom-call | tf_op jit(solution)/shard_map/select/pallas_call | solution.py:88
  42.5 3.4 %collective-permute-start.12 = (bf16[2,4,40,1024]{3,2,1,0:T(8,128)(2,1)}, bf16[2,4,40,1024]{3,2,1,0:T(8,128)(2,1)S(1)}, u32[]{:S(2)}, u32[]{:S(2)}) collective-permute-start(bf16[2,4,40,1024]{3,2,1,0:T(8,128)(2,1)} %get-tuple-element.62), channel_id=1, source_target_pairs={{0,4},{1,5},{2,6},{3,7},{4,8},{5,9},{6,10},{7,11},{8,12},{9,13},{1... | collective-permute-start | bytes 1966088 | tf_op jit(solution)/shard_map/ppermute | solution.py:26
  48.8 6.5 %select.28 = (bf16[2,4,40,1024]{3,2,1,0:T(8,128)(2,1)}, bf16[2,4,40,1024]{3,2,1,0:T(8,128)(2,1)}, bf16[2,4,40,1024]{3,2,1,0:T(8,128)(2,1)}, bf16[2,4,40,1024]{3,...) custom-call(s32[8]{0:T(128)} %pad_add_fusion.dest_ref, ...), custom_call_target="tpu_custom_call" | custom-call | tf_op jit(solution)/shard_map/select/pallas_call | solution.py:88
  55.3 4.5 %collective-permute-done.12 = bf16[2,4,40,1024]{3,2,1,0:T(8,128)(2,1)S(1)} collective-permute-done((bf16[2,4,40,1024]{3,2,1,0:T(8,128)(2,1)}, bf16[2,4,40,1024]{3,2,1,0:T(8,128)(2,1)S(1)}, u32[]{:S(2)}, u32[]{:S(2)}) %collective-permute-start.12) | collective-permute-done | bytes 655392 | tf_op jit(solution)/shard_map/ppermute | solution.py:26
  59.8 15.5 %collective-permute-done.13 = bf16[2,4,40,1024]{3,2,1,0:T(8,128)(2,1)S(1)} collective-permute-done((bf16[2,4,40,1024]{3,2,1,0:T(8,128)(2,1)}, bf16[2,4,40,1024]{3,2,1,0:T(8,128)(2,1)S(1)}, u32[]{:S(2)}, u32[]{:S(2)}) %collective-permute-start.13) | collective-permute-done | bytes 655392 | tf_op jit(solution)/shard_map/ppermute | solution.py:26
  78.0 3.3 %collective-permute-start.7 = (bf16[2,4,40,1024]{3,2,1,0:T(8,128)(2,1)}, bf16[2,4,40,1024]{3,2,1,0:T(8,128)(2,1)S(1)}, u32[]{:S(2)}, u32[]{:S(2)}) collective-permute-start(bf16[2,4,40,1024]{3,2,1,0:T(8,128)(2,1)} %get-tuple-element.54), channel_id=1, source_target_pairs={{0,8},{1,9},{2,10},{3,11},{4,12},{5,13},{6,14},{7,15},{8,0},{9,1},... | collective-permute-start | bytes 1966088 | tf_op jit(solution)/shard_map/ppermute | solution.py:26
  81.4 26.1 %collective-permute-done.9 = bf16[2,4,40,1024]{3,2,1,0:T(8,128)(2,1)S(1)} collective-permute-done((bf16[2,4,40,1024]{3,2,1,0:T(8,128)(2,1)}, bf16[2,4,40,1024]{3,2,1,0:T(8,128)(2,1)S(1)}, u32[]{:S(2)}, u32[]{:S(2)}) %collective-permute-start.9) | collective-permute-done | bytes 655392 | tf_op jit(solution)/shard_map/ppermute | solution.py:26
  107.5 11.2 %experts.3 = (bf16[2,176,512]{2,1,0:T(8,128)(2,1)}, bf16[2,176,512]{2,1,0:T(8,128)(2,1)}, bf16[2,176,512]{2,1,0:T(8,128)(2,1)}, bf16[2,176,512]{2,1,0:T(8,128)(2...) custom-call(bf16[2,160,1024]{2,1,0:T(8,128)(2,1)} %bitcast.60, ...), custom_call_target="tpu_custom_call" | custom-call | tf_op jit(solution)/shard_map/experts/pallas_call | solution.py:183
  123.2 10.9 %experts.2 = (bf16[2,176,512]{2,1,0:T(8,128)(2,1)}, bf16[2,176,512]{2,1,0:T(8,128)(2,1)}, bf16[2,176,512]{2,1,0:T(8,128)(2,1)}, bf16[2,176,512]{2,1,0:T(8,128)(2...) custom-call(bf16[2,160,1024]{2,1,0:T(8,128)(2,1)} %bitcast.56, ...), custom_call_target="tpu_custom_call" | custom-call | tf_op jit(solution)/shard_map/experts/pallas_call | solution.py:183
  140.3 4.7 %collective-permute-start.23 = (bf16[2,176,512]{2,1,0:T(8,128)(2,1)}, bf16[2,176,512]{2,1,0:T(8,128)(2,1)S(1)}, u32[]{:S(2)}, u32[]{:S(2)}) collective-permute-start(bf16[2,176,512]{2,1,0:T(8,128)(2,1)} %get-tuple-element.75), channel_id=1, source_target_pairs={{0,4},{1,5},{2,6},{3,7},{4,8},{5,9},{6,10},{7,11},{8,12},{9,13},{1... | collective-permute-start | bytes 1081352 | tf_op jit(solution)/shard_map/ppermute | solution.py:26
  145.1 7.2 %collective-permute-done.28.refs_16_ = bf16[2,4,40,512]{3,2,1,0:T(8,128)(2,1)S(1)} collective-permute-done((bf16[2,4,40,512]{3,2,1,0:T(8,128)(2,1)}, bf16[2,4,40,512]{3,2,1,0:T(8,128)(2,1)S(1)}, u32[]{:S(2)}, u32[]{:S(2)}) %collective-permute-start.28) | collective-permute-done | bytes 327712 | tf_op jit(solution)/shard_map/ppermute | solution.py:26
  152.3 3.4 %collective-permute-start.20 = (bf16[2,176,512]{2,1,0:T(8,128)(2,1)}, bf16[2,176,512]{2,1,0:T(8,128)(2,1)}, u32[]{:S(2)}, u32[]{:S(2)}) collective-permute-start(bf16[2,176,512]{2,1,0:T(8,128)(2,1)} %get-tuple-element.72), channel_id=1, source_target_pairs={{0,8},{1,9},{2,10},{3,11},{4,12},{5,13},{6,14},{7,15},{8,0},{9,1},... | collective-permute-start | bytes 1081352 | tf_op jit(solution)/shard_map/ppermute | solution.py:26
  156.1 3.8 %spreads.1 = (bf16[4,256,640]{2,1,0:T(8,128)(2,1)}, bf16[4,256,640]{2,1,0:T(8,128)(2,1)}) custom-call(s32[8]{0:T(128)} %pad_add_fusion.dest_ref, bf16[264,1024]{1,0:T(8,128)(2,1)} %copy-done.1, bf16[264,1024]{1,0:T(8,128)(2,1)} %copy-done.3, bf16[264,1024]{1,0:T(8,128)(2,1)} %collective-permute-done.1.refs_2_, ...), custom_call_target="tpu_custom_call" | custom-call | tf_op jit(solution)/shard_map/spreads/pallas_call | solution.py:126
  159.9 5.1 %collective-permute-done.20.refs_6_ = bf16[2,176,512]{2,1,0:T(8,128)(2,1)} collective-permute-done((bf16[2,176,512]{2,1,0:T(8,128)(2,1)}, bf16[2,176,512]{2,1,0:T(8,128)(2,1)}, u32[]{:S(2)}, u32[]{:S(2)}) %collective-permute-start.20) | collective-permute-done | bytes 360480 | tf_op jit(solution)/shard_map/ppermute | solution.py:26
  165.1 8.9 %collective-permute-done.22.refs_8_.refs_7_ = bf16[2,176,512]{2,1,0:T(8,128)(2,1)} collective-permute-done((bf16[2,176,512]{2,1,0:T(8,128)(2,1)}, bf16[2,176,512]{2,1,0:T(8,128)(2,1)}, u32[]{:S(2)}, u32[]{:S(2)}) %collective-permute-start.22) | collective-permute-done | bytes 360480 | tf_op jit(solution)/shard_map/ppermute | solution.py:26
  174.0 7.0 %combine.1 = (bf16[256,512]{1,0:T(8,128)(2,1)}, bf16[256,512]{1,0:T(8,128)(2,1)}, bf16[256,512]{1,0:T(8,128)(2,1)}, bf16[256,512]{1,0:T(8,128)(2,1)}, bf16[256,5...) custom-call(bf16[4,256,640]{2,1,0:T(8,128)(2,1)} %get-tuple-element.50.refs_0_, ...), custom_call_target="tpu_custom_call" | custom-call | tf_op jit(solution)/shard_map/combine/pallas_call | solution.py:233
  184.6 4.1 %collective-permute-done.30.refs_1_ = bf16[256,512]{1,0:T(8,128)(2,1)S(1)} collective-permute-done((bf16[256,512]{1,0:T(8,128)(2,1)}, bf16[256,512]{1,0:T(8,128)(2,1)S(1)}, u32[]{:S(2)}, u32[]{:S(2)}) %collective-permute-start.30) | collective-permute-done | bytes 262176 | tf_op jit(solution)/shard_map/ppermute | solution.py:26
  188.7 7.5 %convert_bitcast_fusion = bf16[1,4,1024,384]{3,2,1,0:T(8,128)(2,1)} fusion(bf16[1,4,640,1024]{3,2,1,0:T(8,128)(2,1)} %param.18, bf16[4,640]{1,0:T(4,128)(2,1)S(1)} %compare_convert_fusion, bf16[1,4,640,384]{3,2,1,0:T(8,128)(2,1)S(1)} %copy-done), kind=kOutput, calls=%fused_computation.3 | convolution fusion | flops 2017460224 | bytes 10359808 | tf_op jit(solution)/shard_map/esd,esf->edf/dot_general | solution.py:331
  202.0 6.6 %collective-permute-start.36 = (bf16[1,256,1024]{2,1,0:T(8,128)(2,1)}, bf16[1,256,1024]{2,1,0:T(8,128)(2,1)S(1)}, u32[]{:S(2)}, u32[]{:S(2)}) collective-permute-start(bf16[1,256,1024]{2,1,0:T(8,128)(2,1)} %finish.1), channel_id=1, source_target_pairs={{16,0},{32,16},{48,32},{64,48},{80,64},{96,80},{112,96},{17,1},{33... | collective-permute-start | bytes 1572872 | tf_op jit(solution)/shard_map/ppermute | solution.py:395
  208.6 8.1 %convert_bitcast_fusion.1 = bf16[1,4,1024,384]{3,2,1,0:T(8,128)(2,1)} fusion(bf16[1,4,640,1024]{3,2,1,0:T(8,128)(2,1)} %param.18, bf16[4,640]{1,0:T(4,128)(2,1)S(1)} %compare_convert_fusion, bf16[1,4,640,384]{3,2,1,0:T(8,128)(2,1)} %param.19), kind=kOutput, calls=%fused_computation.4 | convolution fusion | flops 2017460224 | bytes 10359808 | tf_op jit(solution)/shard_map/esd,esf->edf/dot_general | solution.py:331
  (147 shorter events, 53.7 us)
Async XLA Ops:
  2.9 16.7 %collective-permute-start = (bf16[264,1024]{1,0:T(8,128)(2,1)S(1)}, bf16[264,1024]{1,0:T(8,128)(2,1)S(1)}, u32[]{:S(2)}, u32[]{:S(2)}) collective-permute-start(bf16[264,1024]{1,0:T(8,128)(2,1)S(1)} %get-tuple-element.97.refs_0_.meta), channel_id=1, source_target_pairs={{0,1},{1,2},{2,3},{3,0},{4,5},{5,6},{6,7},{7,4},{8,9},{9,10},{10,1... | collective-permute-start | bytes 1622024 | tf_op jit(solution)/shard_map/ppermute | solution.py:26
  5.4 26.7 %collective-permute-start.1 = (bf16[264,1024]{1,0:T(8,128)(2,1)S(1)}, bf16[264,1024]{1,0:T(8,128)(2,1)}, u32[]{:S(2)}, u32[]{:S(2)}) collective-permute-start(bf16[264,1024]{1,0:T(8,128)(2,1)S(1)} %get-tuple-element.97.refs_0_.meta), channel_id=1, source_target_pairs={{0,2},{1,3},{2,0},{3,1},{4,6},{5,7},{6,4},{7,5},{8,10},{9,11},{10,... | collective-permute-start | bytes 1622024 | tf_op jit(solution)/shard_map/ppermute | solution.py:26
  8.7 23.4 %collective-permute-start.2 = (bf16[264,1024]{1,0:T(8,128)(2,1)S(1)}, bf16[264,1024]{1,0:T(8,128)(2,1)}, u32[]{:S(2)}, u32[]{:S(2)}) collective-permute-start(bf16[264,1024]{1,0:T(8,128)(2,1)S(1)} %get-tuple-element.97.refs_0_.meta), channel_id=1, source_target_pairs={{0,3},{1,0},{2,1},{3,2},{4,7},{5,4},{6,5},{7,6},{8,11},{9,8},{10,9... | collective-permute-start | bytes 1622024 | tf_op jit(solution)/shard_map/ppermute | solution.py:26
  9.4 22.7 %collective-permute-start.3 = (bf16[264,1024]{1,0:T(8,128)(2,1)S(1)}, bf16[264,1024]{1,0:T(8,128)(2,1)}, u32[]{:S(2)}, u32[]{:S(2)}) collective-permute-start(bf16[264,1024]{1,0:T(8,128)(2,1)S(1)} %get-tuple-element.96.refs_4_), channel_id=1, source_target_pairs={{0,4},{1,5},{2,6},{3,7},{4,8},{5,9},{6,10},{7,11},{8,12},{9,13},{1... | collective-permute-start | bytes 1622024 | tf_op jit(solution)/shard_map/ppermute | solution.py:26
  10.7 25.2 %collective-permute-start.4 = (bf16[264,1024]{1,0:T(8,128)(2,1)S(1)}, bf16[264,1024]{1,0:T(8,128)(2,1)}, u32[]{:S(2)}, u32[]{:S(2)}) collective-permute-start(bf16[264,1024]{1,0:T(8,128)(2,1)S(1)} %get-tuple-element.96.refs_4_), channel_id=1, source_target_pairs={{0,8},{1,9},{2,10},{3,11},{4,12},{5,13},{6,14},{7,15},{8,0},{9,1},... | collective-permute-start | bytes 1622024 | tf_op jit(solution)/shard_map/ppermute | solution.py:26
  42.5 17.3 %collective-permute-start.12 = (bf16[2,4,40,1024]{3,2,1,0:T(8,128)(2,1)}, bf16[2,4,40,1024]{3,2,1,0:T(8,128)(2,1)S(1)}, u32[]{:S(2)}, u32[]{:S(2)}) collective-permute-start(bf16[2,4,40,1024]{3,2,1,0:T(8,128)(2,1)} %get-tuple-element.62), channel_id=1, source_target_pairs={{0,4},{1,5},{2,6},{3,7},{4,8},{5,9},{6,10},{7,11},{8,12},{9,13},{1... | collective-permute-start | bytes 1966088 | tf_op jit(solution)/shard_map/ppermute | solution.py:26
  45.9 29.4 %collective-permute-start.13 = (bf16[2,4,40,1024]{3,2,1,0:T(8,128)(2,1)}, bf16[2,4,40,1024]{3,2,1,0:T(8,128)(2,1)S(1)}, u32[]{:S(2)}, u32[]{:S(2)}) collective-permute-start(bf16[2,4,40,1024]{3,2,1,0:T(8,128)(2,1)} %get-tuple-element.63), channel_id=1, source_target_pairs={{0,8},{1,9},{2,10},{3,11},{4,12},{5,13},{6,14},{7,15},{8,0},{9,1},... | collective-permute-start | bytes 1966088 | tf_op jit(solution)/shard_map/ppermute | solution.py:26
  47.3 28.0 %collective-permute-start.14 = (bf16[2,4,40,1024]{3,2,1,0:T(8,128)(2,1)}, bf16[2,4,40,1024]{3,2,1,0:T(8,128)(2,1)}, u32[]{:S(2)}, u32[]{:S(2)}) collective-permute-start(bf16[2,4,40,1024]{3,2,1,0:T(8,128)(2,1)} %get-tuple-element.64), channel_id=1, source_target_pairs={{0,12},{1,13},{2,14},{3,15},{4,0},{5,1},{6,2},{7,3},{8,4},{9,5},{1... | collective-permute-start | bytes 1966088 | tf_op jit(solution)/shard_map/ppermute | solution.py:26
  48.4 27.0 %collective-permute-start.15 = (bf16[2,4,40,1024]{3,2,1,0:T(8,128)(2,1)}, bf16[2,4,40,1024]{3,2,1,0:T(8,128)(2,1)}, u32[]{:S(2)}, u32[]{:S(2)}) collective-permute-start(bf16[2,4,40,1024]{3,2,1,0:T(8,128)(2,1)} %get-tuple-element.66), channel_id=1, source_target_pairs={{0,1},{1,2},{2,3},{3,0},{4,5},{5,6},{6,7},{7,4},{8,9},{9,10},{10,1... | collective-permute-start | bytes 1966088 | tf_op jit(solution)/shard_map/ppermute | solution.py:26
  48.4 29.7 %collective-permute-start.16 = (bf16[2,4,40,1024]{3,2,1,0:T(8,128)(2,1)}, bf16[2,4,40,1024]{3,2,1,0:T(8,128)(2,1)}, u32[]{:S(2)}, u32[]{:S(2)}) collective-permute-start(bf16[2,4,40,1024]{3,2,1,0:T(8,128)(2,1)} %get-tuple-element.67), channel_id=1, source_target_pairs={{0,2},{1,3},{2,0},{3,1},{4,6},{5,7},{6,4},{7,5},{8,10},{9,11},{10,... | collective-permute-start | bytes 1966088 | tf_op jit(solution)/shard_map/ppermute | solution.py:26
  59.8 18.2 %collective-permute-start.17 = (bf16[2,4,40,1024]{3,2,1,0:T(8,128)(2,1)}, bf16[2,4,40,1024]{3,2,1,0:T(8,128)(2,1)S(1)}, u32[]{:S(2)}, u32[]{:S(2)}) collective-permute-start(bf16[2,4,40,1024]{3,2,1,0:T(8,128)(2,1)} %get-tuple-element.68), channel_id=1, source_target_pairs={{0,3},{1,0},{2,1},{3,2},{4,7},{5,4},{6,5},{7,6},{8,11},{9,8},{10,9... | collective-permute-start | bytes 1966088 | tf_op jit(solution)/shard_map/ppermute | solution.py:26
  75.3 32.2 %collective-permute-start.9 = (bf16[2,4,40,1024]{3,2,1,0:T(8,128)(2,1)}, bf16[2,4,40,1024]{3,2,1,0:T(8,128)(2,1)S(1)}, u32[]{:S(2)}, u32[]{:S(2)}) collective-permute-start(bf16[2,4,40,1024]{3,2,1,0:T(8,128)(2,1)} %get-tuple-element.57), channel_id=1, source_target_pairs={{0,1},{1,2},{2,3},{3,0},{4,5},{5,6},{6,7},{7,4},{8,9},{9,10},{10,1... | collective-permute-start | bytes 1966088 | tf_op jit(solution)/shard_map/ppermute | solution.py:26
  75.3 43.4 %collective-permute-start.10 = (bf16[2,4,40,1024]{3,2,1,0:T(8,128)(2,1)}, bf16[2,4,40,1024]{3,2,1,0:T(8,128)(2,1)S(1)}, u32[]{:S(2)}, u32[]{:S(2)}) collective-permute-start(bf16[2,4,40,1024]{3,2,1,0:T(8,128)(2,1)} %get-tuple-element.58), channel_id=1, source_target_pairs={{0,2},{1,3},{2,0},{3,1},{4,6},{5,7},{6,4},{7,5},{8,10},{9,11},{10,... | collective-permute-start | bytes 1966088 | tf_op jit(solution)/shard_map/ppermute | solution.py:26
  75.4 43.5 %collective-permute-start.11 = (bf16[2,4,40,1024]{3,2,1,0:T(8,128)(2,1)}, bf16[2,4,40,1024]{3,2,1,0:T(8,128)(2,1)S(1)}, u32[]{:S(2)}, u32[]{:S(2)}) collective-permute-start(bf16[2,4,40,1024]{3,2,1,0:T(8,128)(2,1)} %get-tuple-element.59), channel_id=1, source_target_pairs={{0,3},{1,0},{2,1},{3,2},{4,7},{5,4},{6,5},{7,6},{8,11},{9,8},{10,9... | collective-permute-start | bytes 1966088 | tf_op jit(solution)/shard_map/ppermute | solution.py:26
  78.0 40.9 %collective-permute-start.6 = (bf16[2,4,40,1024]{3,2,1,0:T(8,128)(2,1)}, bf16[2,4,40,1024]{3,2,1,0:T(8,128)(2,1)S(1)}, u32[]{:S(2)}, u32[]{:S(2)}) collective-permute-start(bf16[2,4,40,1024]{3,2,1,0:T(8,128)(2,1)} %get-tuple-element.53), channel_id=1, source_target_pairs={{0,4},{1,5},{2,6},{3,7},{4,8},{5,9},{6,10},{7,11},{8,12},{9,13},{1... | collective-permute-start | bytes 1966088 | tf_op jit(solution)/shard_map/ppermute | solution.py:26
  78.0 41.4 %collective-permute-start.7 = (bf16[2,4,40,1024]{3,2,1,0:T(8,128)(2,1)}, bf16[2,4,40,1024]{3,2,1,0:T(8,128)(2,1)S(1)}, u32[]{:S(2)}, u32[]{:S(2)}) collective-permute-start(bf16[2,4,40,1024]{3,2,1,0:T(8,128)(2,1)} %get-tuple-element.54), channel_id=1, source_target_pairs={{0,8},{1,9},{2,10},{3,11},{4,12},{5,13},{6,14},{7,15},{8,0},{9,1},... | collective-permute-start | bytes 1966088 | tf_op jit(solution)/shard_map/ppermute | solution.py:26
  118.7 16.4 %collective-permute-start.25 = (bf16[2,4,40,512]{3,2,1,0:T(8,128)(2,1)}, bf16[2,4,40,512]{3,2,1,0:T(8,128)(2,1)S(1)}, u32[]{:S(2)}, u32[]{:S(2)}) collective-permute-start(bf16[2,4,40,512]{3,2,1,0:T(8,128)(2,1)} %get-tuple-element.79), channel_id=1, source_target_pairs={{0,3},{1,0},{2,1},{3,2},{4,7},{5,4},{6,5},{7,6},{8,11},{9,8},{10,9... | collective-permute-start | bytes 983048 | tf_op jit(solution)/shard_map/ppermute | solution.py:26
  118.8 17.3 %collective-permute-start.27 = (bf16[2,4,40,512]{3,2,1,0:T(8,128)(2,1)}, bf16[2,4,40,512]{3,2,1,0:T(8,128)(2,1)S(1)}, u32[]{:S(2)}, u32[]{:S(2)}) collective-permute-start(bf16[2,4,40,512]{3,2,1,0:T(8,128)(2,1)} %get-tuple-element.81), channel_id=1, source_target_pairs={{0,2},{1,3},{2,0},{3,1},{4,6},{5,7},{6,4},{7,5},{8,10},{9,11},{10,... | collective-permute-start | bytes 983048 | tf_op jit(solution)/shard_map/ppermute | solution.py:26
  119.0 36.8 %collective-permute-start.19 = (bf16[2,176,512]{2,1,0:T(8,128)(2,1)}, bf16[2,176,512]{2,1,0:T(8,128)(2,1)S(1)}, u32[]{:S(2)}, u32[]{:S(2)}) collective-permute-start(bf16[2,176,512]{2,1,0:T(8,128)(2,1)} %get-tuple-element.71), channel_id=1, source_target_pairs={{0,12},{1,13},{2,14},{3,15},{4,0},{5,1},{6,2},{7,3},{8,4},{9,5},{1... | collective-permute-start | bytes 1081352 | tf_op jit(solution)/shard_map/ppermute | solution.py:26
  119.4 17.5 %collective-permute-start.29 = (bf16[2,4,40,512]{3,2,1,0:T(8,128)(2,1)}, bf16[2,4,40,512]{3,2,1,0:T(8,128)(2,1)S(1)}, u32[]{:S(2)}, u32[]{:S(2)}) collective-permute-start(bf16[2,4,40,512]{3,2,1,0:T(8,128)(2,1)} %get-tuple-element.83), channel_id=1, source_target_pairs={{0,1},{1,2},{2,3},{3,0},{4,5},{5,6},{6,7},{7,4},{8,9},{9,10},{10,1... | collective-permute-start | bytes 983048 | tf_op jit(solution)/shard_map/ppermute | solution.py:26
  136.9 23.0 %collective-permute-start.21 = (bf16[2,176,512]{2,1,0:T(8,128)(2,1)}, bf16[2,176,512]{2,1,0:T(8,128)(2,1)S(1)}, u32[]{:S(2)}, u32[]{:S(2)}) collective-permute-start(bf16[2,176,512]{2,1,0:T(8,128)(2,1)} %get-tuple-element.73), channel_id=1, source_target_pairs={{0,8},{1,9},{2,10},{3,11},{4,12},{5,13},{6,14},{7,15},{8,0},{9,1},... | collective-permute-start | bytes 1081352 | tf_op jit(solution)/shard_map/ppermute | solution.py:26
  140.3 19.6 %collective-permute-start.23 = (bf16[2,176,512]{2,1,0:T(8,128)(2,1)}, bf16[2,176,512]{2,1,0:T(8,128)(2,1)S(1)}, u32[]{:S(2)}, u32[]{:S(2)}) collective-permute-start(bf16[2,176,512]{2,1,0:T(8,128)(2,1)} %get-tuple-element.75), channel_id=1, source_target_pairs={{0,4},{1,5},{2,6},{3,7},{4,8},{5,9},{6,10},{7,11},{8,12},{9,13},{1... | collective-permute-start | bytes 1081352 | tf_op jit(solution)/shard_map/ppermute | solution.py:26
  155.8 18.2 %collective-permute-start.22 = (bf16[2,176,512]{2,1,0:T(8,128)(2,1)}, bf16[2,176,512]{2,1,0:T(8,128)(2,1)}, u32[]{:S(2)}, u32[]{:S(2)}) collective-permute-start(bf16[2,176,512]{2,1,0:T(8,128)(2,1)} %get-tuple-element.74), channel_id=1, source_target_pairs={{0,4},{1,5},{2,6},{3,7},{4,8},{5,9},{6,10},{7,11},{8,12},{9,13},{1... | collective-permute-start | bytes 1081352 | tf_op jit(solution)/shard_map/ppermute | solution.py:26
  202.0 28.1 %collective-permute-start.36 = (bf16[1,256,1024]{2,1,0:T(8,128)(2,1)}, bf16[1,256,1024]{2,1,0:T(8,128)(2,1)S(1)}, u32[]{:S(2)}, u32[]{:S(2)}) collective-permute-start(bf16[1,256,1024]{2,1,0:T(8,128)(2,1)} %finish.1), channel_id=1, source_target_pairs={{16,0},{32,16},{48,32},{64,48},{80,64},{96,80},{112,96},{17,1},{33... | collective-permute-start | bytes 1572872 | tf_op jit(solution)/shard_map/ppermute | solution.py:395
  (49 other events, 745.4 us)
where the time goes:
time: 231 us
  waiting for transfers between devices  97.8 us (42%)
  starting transfers between devices  55.2 us (24%)
  Pallas kernels  53.7 us (23%)
  matrix products  15.6 us (7%)
  local copies, waits for them, and re-layouts  4.63 us (2%)
  other arithmetic  2.87 us (1%)
    ppermute x39, waiting for transfers between devices, moved(): return lax.ppermute(array, 'ep', pairs)  97.8 us
    ppermute x39, starting transfers between devices, moved(): return lax.ppermute(array, 'ep', pairs)  48.6 us
    pallas_call x2, Pallas kernels, experts(): pl.pallas_call(expert_body, out_shape=(jax.ShapeDtypeStruct((2, 176, 512)...  22.1 us
    dot_general x2, matrix products, weight_grad(): jnp.einsum('esd,esf->edf', masked, grads, preferred_element_type=F32)  15.6 us
    pallas_call x2, Pallas kernels, select(): pl.pallas_call(functools.partial(select_body, first=first), out_shape=(ou...  13 us
    pallas_call x1, Pallas kernels, combine(): pl.pallas_call(combine_body, out_shape=(jax.ShapeDtypeStruct((256, 512),...  6.97 us
    ppermute x1, starting transfers between devices, per_device(): lax.ppermute(input_grad, 'section', [(s, s - 1) for s in range(1, section...  6.61 us
  transfers between devices with their start and end apart: 40, of which 16 were waited for; matrix products, arithmetic and copies ran while one was open for 7% of the time, Pallas kernels for 16%

commit v1 on v0

v1 whole, which is shorter than its diff:
```python
import functools

import jax
import jax.numpy as jnp
from jax import lax
from jax.experimental import pallas as pl
from jax.experimental.pallas import tpu as pltpu
from jax.sharding import PartitionSpec as P


BF = jnp.bfloat16
F32 = jnp.float32
SIDE = 4
CAP = 40


def along_z(k):
    return [(4 * y + z, 4 * y + (z + k) % 4) for y in range(4) for z in range(4)]


def along_y(k):
    return [(4 * y + z, 4 * ((y + k) % 4) + z) for y in range(4) for z in range(4)]


def in_vmem(arrays):
    return [pltpu.with_memory_space_constraint(a, pltpu.VMEM) for a in arrays]


def in_hbm(arrays):
    return [pltpu.with_memory_space_constraint(a, pltpu.HBM) for a in arrays]


VMEM_SPEC = pl.BlockSpec(memory_space=pltpu.VMEM)
SMEM_SPEC = pl.BlockSpec(memory_space=pltpu.SMEM)


def room(mib):
    return pltpu.CompilerParams(vmem_limit_bytes=mib * 1024 * 1024)


def moved(array, pairs):
    return lax.ppermute(array, "ep", pairs)


def iota(shape, dim):
    return lax.broadcasted_iota(jnp.int32, shape, dim)


def expert_of_row(dest_ref, rows, per_dest, first, base):
    row = iota((rows, 256), 0)
    expert = jnp.zeros((rows, 256), jnp.int32)
    for i in range(SIDE):
        expert = jnp.where(row // per_dest == i, 4 * dest_ref[base + i] + first + row % per_dest, expert)
    return expert.astype(F32)


def earlier():
    return (iota((256, 256), 0) < iota((256, 256), 1)).astype(BF)


def slot_ranks(ids_list, expert, rows):
    marks = []
    for ids in ids_list:
        mark = jnp.zeros((rows, 256), F32)
        for k in range(8):
            mark = mark + jnp.where(ids[k : k + 1, :] == expert, 1.0, 0.0)
        marks.append(mark)
    mark = jnp.concatenate(marks, axis=0)
    rank = jnp.dot(mark.astype(BF), earlier(), preferred_element_type=F32)
    rank = jnp.where(mark > 0.0, rank, -1.0)
    return [rank[rows * j : rows * j + rows] for j in range(len(ids_list))]


def select_own_body(dest_ref, *refs):
    blocks, outs = refs[:2], refs[2:10]
    slot = iota((16, CAP, 256), 1).astype(F32)
    for c in range(2):
        expert = expert_of_row(dest_ref, 16, 4, 0, 4 * c)
        mine = slot_ranks([blocks[c][256:264, 0:256].astype(F32)], expert, 16)[0]
        pick = jnp.where(mine[:, None, :] == slot, 1.0, 0.0).reshape(16 * CAP, 256).astype(BF)
        rows = jnp.dot(pick, blocks[c][0:256, :], preferred_element_type=F32)
        for i in range(SIDE):
            for e in range(4):
                at = (4 * i + e) * CAP
                outs[4 * c + i][e] = rows[at : at + CAP].astype(BF)


def select_own(dest, block_a, block_b):
    outs = pl.pallas_call(
        select_own_body,
        out_shape=(pltpu.VMEM((4, CAP, 1024), BF),) * 8,
        in_specs=[SMEM_SPEC] + [VMEM_SPEC] * 2,
        out_specs=[VMEM_SPEC] * 8,
        compiler_params=room(12),
        name="select_own",
    )(dest, *in_vmem([block_a, block_b]))
    return outs[:4], outs[4:]


def select_body(dest_ref, *refs, first):
    blocks, outs = refs[:6], refs[6:14]
    slot = iota((8, CAP, 256), 1).astype(F32)
    ranks = []
    for c in range(2):
        ids_list = [blocks[3 * c + j][256:264, 0:256].astype(F32) for j in range(3)]
        ranks.append(slot_ranks(ids_list, expert_of_row(dest_ref, 8, 2, first, 4 * c), 8))
    for j in range(3):
        for c in range(2):
            pick = jnp.where(ranks[c][j][:, None, :] == slot, 1.0, 0.0)
            pick = pick.reshape(8 * CAP, 256).astype(BF)
            rows = jnp.dot(pick, blocks[3 * c + j][0:256, :], preferred_element_type=F32)
            for i in range(SIDE):
                for e in range(2):
                    at = (2 * i + e) * CAP
                    outs[4 * c + i][e, j] = rows[at : at + CAP].astype(BF)


def select(dest, blocks_a, blocks_b, first):
    outs = pl.pallas_call(
        functools.partial(select_body, first=first),
        out_shape=(pltpu.VMEM((2, 3, CAP, 1024), BF),) * 8,
        in_specs=[SMEM_SPEC] + [VMEM_SPEC] * 6,
        out_specs=[VMEM_SPEC] * 8,
        compiler_params=room(10),
        name="select",
    )(dest, *in_vmem(blocks_a[1:] + blocks_b[1:]))
    return outs[:4], outs[4:]


def spread_body(dest_ref, *refs):
    metas, outs, rank_ref = refs[:8], refs[8:10], refs[10]
    slot = iota((16, CAP, 256), 1).astype(F32)
    for c in range(2):
        expert = expert_of_row(dest_ref, 16, 4, 0, 4 * c)
        mine = metas[4 * c : 4 * c + 4]
        ids_list = [m[256:264, 0:256].astype(F32) for m in mine]
        ranks = slot_ranks(ids_list, expert, 16)
        for j in range(4):
            weight = mine[j][256:264, 256:512].astype(F32)
            scale = jnp.zeros((16, 256), F32)
            for k in range(8):
                scale = scale + jnp.where(ids_list[j][k : k + 1, :] == expert, weight[k : k + 1, :], 0.0)
            spread = jnp.where(ranks[j][:, None, :] == slot, scale[:, None, :], 0.0).reshape(16 * CAP, 256)
            outs[c][j] = spread.T.astype(BF)
            if c == 0:
                rank_ref[j] = ranks[j]


def spreads(dest, blocks_a, blocks_b):
    return pl.pallas_call(
        spread_body,
        out_shape=(pltpu.VMEM((SIDE, 256, 16 * CAP), BF),) * 2 + (pltpu.VMEM((SIDE, 16, 256), F32),),
        in_specs=[SMEM_SPEC] + [VMEM_SPEC] * 8,
        out_specs=[VMEM_SPEC] * 3,
        compiler_params=room(10),
        name="spreads",
    )(dest, *in_vmem(blocks_a + blocks_b))


def expert_body(*refs, half):
    own_xs, xs, own_gs, gs = (refs[4 * k : 4 * k + 4] for k in range(4))
    wg_ref, wu_ref, wd_ref = refs[16:19]
    a_outs, b_outs = refs[-8:-4], refs[-4:]
    e = pl.program_id(0)

    def joined(own, others):
        pieces = [r.astype(F32) for a, b in zip(own, others) for r in (a[2 * half + e], b[e])]
        return jnp.concatenate(pieces, axis=0).astype(BF)

    rows, grads = joined(own_xs, xs), joined(own_gs, gs)
    wg, wu, wd = wg_ref[0], wu_ref[0], wd_ref[0]
    nt = (((1,), (1,)), ((), ()))
    gate = jnp.dot(rows, wg, preferred_element_type=F32)
    up = jnp.dot(rows, wu, preferred_element_type=F32)
    hg = lax.dot_general(grads, wd, nt, preferred_element_type=F32)
    hg = jnp.concatenate(
        [hg[(4 * j + i) * CAP : (4 * j + i + 1) * CAP] for i in range(4) for j in range(4)], axis=0
    )
    sigma = jax.nn.sigmoid(gate)
    active = gate * sigma
    hidden = (active * up).astype(BF).astype(F32)
    prob = jnp.sum(hidden * hg, axis=1, keepdims=True)
    gate_grad = (hg * up * sigma * (1.0 + gate * (1.0 - sigma))).astype(BF)
    up_grad = (hg * active).astype(BF)
    lane = iota((CAP, 128), 1)
    for i in range(4):
        mine = jnp.zeros((CAP, 128), F32)
        for j in range(4):
            at = (4 * i + j) * CAP
            mine = jnp.where(lane == j, prob[at : at + CAP], mine)
        for t in range(5):
            a_outs[i][e, 160 + 8 * (t // 4) : 168 + 8 * (t // 4), 128 * (t % 4) : 128 * (t % 4) + 128] = mine[
                8 * t : 8 * t + 8
            ].astype(BF)
    back = lax.dot_general(gate_grad, wg, nt, preferred_element_type=F32)
    back = back + lax.dot_general(up_grad, wu, nt, preferred_element_type=F32)
    for i in range(4):
        for j in range(4):
            at = (4 * i + j) * CAP
            a_outs[i][e, CAP * j : CAP * j + CAP, :] = back[at : at + CAP, 0:512].astype(BF)
            b_outs[j][e, i] = back[at : at + CAP, 512:1024].astype(BF)


def experts(own_xs, xs, own_gs, gs, w_gate, w_up, w_down, half):
    w_in = pl.BlockSpec((1, 1024, 384), lambda e: (2 * half + e, 0, 0))
    w_out = pl.BlockSpec((1, 384, 1024), lambda e: (2 * half + e, 0, 0))
    xs, gs = ([a.reshape(2, 120, 1024) for a in part] for part in (xs, gs))
    outs = pl.pallas_call(
        functools.partial(expert_body, half=half),
        out_shape=(pltpu.VMEM((2, 176, 512), BF),) * 4 + (pltpu.VMEM((2, SIDE, CAP, 512), BF),) * 4,
        grid=(2,),
        in_specs=[VMEM_SPEC] * 16 + [w_in, w_in, w_out],
        out_specs=[VMEM_SPEC] * 8,
        compiler_params=room(28),
        name="experts",
    )(*in_vmem([*own_xs, *xs, *own_gs, *gs]), w_gate, w_up, w_down)
    return outs[0:4], outs[4:8]


def values_at_tokens(rank, columns, j):
    slot = iota((CAP, 256), 0).astype(F32)
    found = []
    for r in range(16):
        one = jnp.where(rank[r : r + 1] == slot, columns[r][:, j : j + 1], 0.0)
        found.append(jnp.sum(one, axis=0, keepdims=True))
    return jnp.concatenate(found, axis=0)


def combine_body(*refs):
    rank_ref, weights, rows_in, outs = refs[0], refs[1:3], refs[3:19], refs[19:27]
    columns = []
    for source in rows_in[0:8]:
        for e in range(2):
            tile = [
                source[e, 160 + 8 * (t // 4) : 168 + 8 * (t // 4), 128 * (t % 4) : 128 * (t % 4) + 128]
                for t in range(5)
            ]
            columns.append(jnp.concatenate([t.astype(F32) for t in tile], axis=0))
    for j in range(4):
        for c in range(2):
            pieces = []
            for source in rows_in[8 * c : 8 * c + 8]:
                for e in range(2):
                    pieces.append(source[e, CAP * j : CAP * j + CAP] if c == 0 else source[e, j])
            joined = jnp.concatenate([p.astype(F32) for p in pieces], axis=0).astype(BF)
            out = outs[4 * c + j]
            out[0:256, :] = jnp.dot(weights[c][j], joined, preferred_element_type=F32).astype(BF)
            if c == 0:
                values = values_at_tokens(rank_ref[j], columns, j)
                out[256:264, 0:256] = values[0:8].astype(BF)
                out[256:264, 256:512] = values[8:16].astype(BF)


def combine(ranks, spread_a, spread_b, lows, highs):
    both = [pair[half][i] for pair in (lows, highs) for i in range(4) for half in range(2)]
    outs = pl.pallas_call(
        combine_body,
        out_shape=(pltpu.VMEM((264, 512), BF),) * 4 + (pltpu.VMEM((256, 512), BF),) * 4,
        in_specs=[VMEM_SPEC] * 19,
        out_specs=[VMEM_SPEC] * 8,
        compiler_params=room(12),
        name="combine",
    )(*in_vmem([ranks, spread_a, spread_b, *both]))
    return outs[0:4], outs[4:8]


def pick_probs_body(place_ref, meta, *refs):
    tables, prob_ref = refs[0:4], refs[4]
    ids = meta[256:264, 0:256].astype(F32)
    found = [jnp.zeros((8, 256), F32) for _ in range(8)]
    row = iota((8, 256), 0)
    for j in range(4):
        for part in range(2):
            values = tables[j][256:264, 256 * part : 256 * part + 256].astype(F32)
            at = 4 * j + 2 * part
            device = jnp.where(row // 4 == 0, place_ref[at], place_ref[at + 1])
            expert = (4 * device + row % 4).astype(F32)
            for k in range(8):
                found[k] = found[k] + jnp.where(ids[k : k + 1, :] == expert, values, 0.0)
    rows = [jnp.sum(f, axis=0, keepdims=True) for f in found]
    prob_ref[...] = jnp.concatenate(rows, axis=0).astype(BF)


def pick_probs(places, block, tables):
    return pl.pallas_call(
        pick_probs_body,
        out_shape=jax.ShapeDtypeStruct((8, 256), BF),
        in_specs=[SMEM_SPEC] + [VMEM_SPEC] * 5,
        compiler_params=room(4),
        name="pick_probs",
    )(places, *in_vmem([block, *tables]))


def finish_body(*refs):
    left, right, out_ref = refs[0:4], refs[4:8], refs[8]
    for at, parts in ((0, left), (512, right)):
        total = parts[0][0:256, :].astype(F32)
        for part in parts[1:]:
            total = total + part[0:256, :].astype(F32)
        out_ref[0, :, at : at + 512] = total.astype(BF)


def finish(left, right):
    return pl.pallas_call(
        finish_body,
        out_shape=pltpu.VMEM((1, 256, 1024), BF),
        in_specs=[VMEM_SPEC] * 8,
        out_specs=VMEM_SPEC,
        compiler_params=room(6),
        name="finish",
    )(*in_vmem(left), *in_vmem(right))


def weight_grads_body(count_ref, x_ref, gate_ref, up_ref, *refs, first):
    gate_out, up_out = refs[-2:]
    e = first + pl.program_id(0)
    slot = iota((CAP, 384), 0)
    gate, up = [], []
    for source in range(16):
        live = slot < count_ref[16 * e + source]
        at = CAP * source
        gate.append(jnp.where(live, gate_ref[0, at : at + CAP].astype(F32), 0.0))
        up.append(jnp.where(live, up_ref[0, at : at + CAP].astype(F32), 0.0))
    tn = (((0,), (0,)), ((), ()))
    for out, parts in ((gate_out, gate), (up_out, up)):
        grads = jnp.concatenate(parts, axis=0).astype(BF)
        out[0] = lax.dot_general(x_ref[0], grads, tn, preferred_element_type=F32).astype(BF)


def weight_grads(counts, inputs, gate, up, first, before=()):
    out = jax.ShapeDtypeStruct((4, 1024, 384), BF)
    anywhere = pl.BlockSpec(memory_space=pl.ANY)
    return pl.pallas_call(
        functools.partial(weight_grads_body, first=first),
        out_shape=(out, out),
        grid_spec=pltpu.PrefetchScalarGridSpec(
            num_scalar_prefetch=1,
            grid=(2,),
            in_specs=[pl.BlockSpec((1, 640, 1024), lambda g, c: (first + g, 0, 0))]
            + [pl.BlockSpec((1, 640, 384), lambda g, c: (first + g, 0, 0))] * 2
            + [anywhere] * len(before),
            out_specs=[pl.BlockSpec((1, 1024, 384), lambda g, c: (first + g, 0, 0))] * 2,
        ),
        input_output_aliases={4: 0, 5: 1} if before else {},
        compiler_params=room(20),
        name="weight_grads",
    )(counts, *in_hbm([inputs, gate, up]), *before)


ORDER = (2, 1, 3)


def spread_out(arrays, pairs_of, sign=1):
    out = {0: arrays[0]}
    for k in ORDER:
        out[k] = moved(arrays[k], pairs_of(sign * k))
    return [out[k] for k in range(4)]


def per_device(
    output_grad,
    layer_input,
    expert_ids,
    route_probs,
    gate_weight,
    up_weight,
    down_weight,
    saved_inputs,
    saved_gate_grad,
    saved_up_grad,
    saved_counts,
):
    here = lax.axis_index("ep").astype(jnp.int32)
    sections = lax.axis_size("section")
    y, z = here // 4, here % 4
    steps = jnp.arange(4, dtype=jnp.int32)
    column = 4 * ((y + steps) % 4) + z
    row = 4 * y + (z + steps) % 4
    dest = jnp.concatenate([column, row])
    places = (4 * ((y + steps) % 4)[None, :] + ((z + steps) % 4)[:, None]).reshape(16)
    w_gate, w_up, w_down = gate_weight[0], up_weight[0], down_weight[0]

    meta = jnp.concatenate(
        [expert_ids[0].T.astype(BF), route_probs[0].T, jnp.zeros((8, 512), BF)], axis=1
    )
    block_a = jnp.concatenate([layer_input[0], meta], axis=0)
    block_b = jnp.concatenate([output_grad[0], meta], axis=0)
    blocks_a = spread_out([block_a] * 4, along_z)
    blocks_b = spread_out([block_b] * 4, along_y)

    saved = (saved_counts[0].reshape(-1), saved_inputs[0], saved_gate_grad[0], saved_up_grad[0])
    partly = weight_grads(*saved, 0)
    gate_part, up_part = weight_grads(*saved, 2, partly)

    sent_a, sent_b = select_own(dest, block_a, block_b)
    own_xs = spread_out(sent_a, along_y)
    own_gs = spread_out(sent_b, along_z)
    lows, highs = [], []
    for half in range(2):
        sent_a, sent_b = select(dest, blocks_a, blocks_b, 2 * half)
        xs = spread_out(sent_a, along_y)
        gs = spread_out(sent_b, along_z)
        back_a, back_b = experts(own_xs, xs, own_gs, gs, w_gate, w_up, w_down, half)
        lows.append(spread_out(back_a, along_y, -1))
        highs.append(spread_out(back_b, along_z, -1))
    spread_a, spread_b, ranks = spreads(dest, blocks_a, blocks_b)
    made_a, made_b = combine(ranks, spread_a, spread_b, lows, highs)
    left = spread_out(made_a, along_z, -1)
    right = spread_out(made_b, along_y, -1)
    input_grad = finish(left, right)
    upstream = lax.ppermute(input_grad, "section", [(s, s - 1) for s in range(1, sections)])
    prob_rows = pick_probs(places, block_a, left)
    return (upstream, prob_rows.T[None], gate_part[None], up_part[None])


def solution(mesh):
    rows = P("section", "ep", None)
    stacks = P("section", "ep", None, None)

    return jax.shard_map(
        per_device,
        mesh=mesh,
        in_specs=(rows, rows, rows, rows) + (stacks,) * 6 + (rows,),
        out_specs=(rows, rows, stacks, stacks),
        check_vma=False,
    )
```

time: 231 us -> 203 us (0.88)
  waiting for transfers between devices: 97.8 us -> 71.5 us
  starting transfers between devices: 55.2 us -> 80.8 us
  matrix products: 15.6 us -> 0 us
  Pallas kernels: 53.7 us -> 43.8 us
    ppermute x39 -> x42, starting transfers between devices: 48.6 us -> 78.1 us  [moved(): return lax.ppermute(array, 'ep', pairs)]
    ppermute x39 -> x42, waiting for transfers between devices: 97.8 us -> 71.5 us  [moved(): return lax.ppermute(array, 'ep', pairs)]
    dot_general x2 -> x0, matrix products: 15.6 us -> none  [weight_grad(): jnp.einsum('esd,esf->edf', masked, grads, preferred_element_type=F32)]
    pallas_call x8 -> x10, Pallas kernels: 51.6 us -> 42.1 us  [the longest x2 15.3 us: experts(): pl.pallas_call(functools.partial(expert_body, half=half), out_shape=(pltp...]
    ppermute x1, starting transfers between devices: 6.61 us -> 2.74 us  [per_device(): lax.ppermute(input_grad, 'section', [(s, s - 1) for s in range(1, section...]
  transfers between devices with their start and end apart: 40 -> 43, of which waited for: 16 -> 15; matrix products, arithmetic and copies ran while one was open for 7% -> 0% of each run, Pallas kernels for 16% -> 21%
where the time goes in v1:
time: 203 us
  starting transfers between devices  80.8 us (40%)
  waiting for transfers between devices  71.5 us (35%)
  Pallas kernels  43.8 us (22%)
  other arithmetic  3.37 us (2%)
  local copies, waits for them, and re-layouts  2.83 us (1%)
    ppermute x42, starting transfers between devices, moved(): return lax.ppermute(array, 'ep', pairs)  78.1 us
    ppermute x42, waiting for transfers between devices, moved(): return lax.ppermute(array, 'ep', pairs)  71.5 us
    pallas_call x2, Pallas kernels, experts(): pl.pallas_call(functools.partial(expert_body, half=half), out_shape=(pltp...  15.3 us
    pallas_call x2, Pallas kernels, weight_grads(): pl.pallas_call(functools.partial(weight_grads_body, first=first), out_sha...  12.9 us
    pallas_call x2, Pallas kernels, select(): pl.pallas_call(functools.partial(select_body, first=first), out_shape=(pl...  6.18 us
  transfers between devices with their start and end apart: 43, of which 15 were waited for; matrix products, arithmetic and copies ran while one was open for 0% of the time, Pallas kernels for 21%

profile of v1, /device:TPU:1, one launch (start us, length us, event | category | flops | bytes accessed | tf_op | source)
XLA Modules:
  0.0 203.1 jit_solution(762041057676701136)
XLA Ops:
  3.8 3.6 %collective-permute-start.5 = (bf16[264,1024]{1,0:T(8,128)(2,1)}, bf16[264,1024]{1,0:T(8,128)(2,1)S(1)}, u32[]{:S(2)}, u32[]{:S(2)}) collective-permute-start(bf16[264,1024]{1,0:T(8,128)(2,1)} %get-tuple-element.114.refs_4_.refs_1_), channel_id=1, source_target_pairs={{0,12},{1,13},{2,14},{3,15},{4,0},{5,1},{6,2},{7,3},{8,4},{9,5},{1... | collective-permute-start | bytes 1622024 | tf_op jit(solution)/shard_map/ppermute | solution.py:42
  8.4 3.8 %collective-permute-start.2 = (bf16[264,1024]{1,0:T(8,128)(2,1)}, bf16[264,1024]{1,0:T(8,128)(2,1)}, u32[]{:S(2)}, u32[]{:S(2)}) collective-permute-start(bf16[264,1024]{1,0:T(8,128)(2,1)} %get-tuple-element.115.refs_0_.meta), channel_id=1, source_target_pairs={{0,3},{1,0},{2,1},{3,2},{4,7},{5,4},{6,5},{7,6},{8,11},{9,8},{10,9... | collective-permute-start | bytes 1622024 | tf_op jit(solution)/shard_map/ppermute | solution.py:42
  12.2 17.9 %collective-permute-done.5.refs_7_.refs_5_ = bf16[264,1024]{1,0:T(8,128)(2,1)S(1)} collective-permute-done((bf16[264,1024]{1,0:T(8,128)(2,1)}, bf16[264,1024]{1,0:T(8,128)(2,1)S(1)}, u32[]{:S(2)}, u32[]{:S(2)}) %collective-permute-start.5) | collective-permute-done | bytes 540704 | tf_op jit(solution)/shard_map/ppermute | solution.py:42
  35.0 4.7 %collective-permute-start.7 = (bf16[4,40,1024]{2,1,0:T(8,128)(2,1)S(1)}, bf16[4,40,1024]{2,1,0:T(8,128)(2,1)S(1)}, u32[]{:S(2)}, u32[]{:S(2)}) collective-permute-start(bf16[4,40,1024]{2,1,0:T(8,128)(2,1)S(1)} %get-tuple-element.64), channel_id=1, source_target_pairs={{0,8},{1,9},{2,10},{3,11},{4,12},{5,13},{6,14},{7,15},{8,0},{9,1},... | collective-permute-start | bytes 983048 | tf_op jit(solution)/shard_map/ppermute | solution.py:42
  49.0 3.7 %collective-permute-done.7.refs_2_ = bf16[4,40,1024]{2,1,0:T(8,128)(2,1)S(1)} collective-permute-done((bf16[4,40,1024]{2,1,0:T(8,128)(2,1)S(1)}, bf16[4,40,1024]{2,1,0:T(8,128)(2,1)S(1)}, u32[]{:S(2)}, u32[]{:S(2)}) %collective-permute-start.7) | collective-permute-done | bytes 327712 | tf_op jit(solution)/shard_map/ppermute | solution.py:42
  52.7 3.4 %collective-permute-start.19 = (bf16[2,3,40,1024]{3,2,1,0:T(8,128)(2,1)S(1)}, bf16[2,3,40,1024]{3,2,1,0:T(8,128)(2,1)S(1)}, u32[]{:S(2)}, u32[]{:S(2)}) collective-permute-start(bf16[2,3,40,1024]{3,2,1,0:T(8,128)(2,1)S(1)} %get-tuple-element.81), channel_id=1, source_target_pairs={{0,8},{1,9},{2,10},{3,11},{4,12},{5,13},{6,14},{7,15},{8,0},{9,1},... | collective-permute-start | bytes 1474568 | tf_op jit(solution)/shard_map/ppermute | solution.py:42
  68.7 4.5 %collective-permute-done.19 = bf16[2,3,40,1024]{3,2,1,0:T(8,128)(2,1)S(1)} collective-permute-done((bf16[2,3,40,1024]{3,2,1,0:T(8,128)(2,1)S(1)}, bf16[2,3,40,1024]{3,2,1,0:T(8,128)(2,1)S(1)}, u32[]{:S(2)}, u32[]{:S(2)}) %collective-permute-start.19) | collective-permute-done | bytes 491552 | tf_op jit(solution)/shard_map/ppermute | solution.py:42
  80.3 5.0 %collective-permute-done.23 = bf16[2,3,40,1024]{3,2,1,0:T(8,128)(2,1)S(1)} collective-permute-done((bf16[2,3,40,1024]{3,2,1,0:T(8,128)(2,1)S(1)}, bf16[2,3,40,1024]{3,2,1,0:T(8,128)(2,1)S(1)}, u32[]{:S(2)}, u32[]{:S(2)}) %collective-permute-start.23) | collective-permute-done | bytes 491552 | tf_op jit(solution)/shard_map/ppermute | solution.py:42
  89.4 7.7 %experts.3 = (bf16[2,176,512]{2,1,0:T(8,128)(2,1)S(1)}, bf16[2,176,512]{2,1,0:T(8,128)(2,1)S(1)}, bf16[2,176,512]{2,1,0:T(8,128)(2,1)S(1)}, bf16[2,176,512]{2,1,...) custom-call(bf16[4,40,1024]{2,1,0:T(8,128)(2,1)S(1)} %get-tuple-elem, ...), custom_call_target="tpu_custom_call" | custom-call | tf_op jit(solution)/shard_map/experts/pallas_call | solution.py:208
  97.9 3.5 %collective-permute-start.33 = (bf16[2,4,40,512]{3,2,1,0:T(8,128)(2,1)S(1)}, bf16[2,4,40,512]{3,2,1,0:T(8,128)(2,1)S(1)}, u32[]{:S(2)}, u32[]{:S(2)}) collective-permute-start(bf16[2,4,40,512]{3,2,1,0:T(8,128)(2,1)S(1)} %get-tuple-element.99), channel_id=1, source_target_pairs={{0,2},{1,3},{2,0},{3,1},{4,6},{5,7},{6,4},{7,5},{8,10},{9,11},{10,... | collective-permute-start | bytes 983048 | tf_op jit(solution)/shard_map/ppermute | solution.py:42
  101.4 4.0 %collective-permute-start.25 = (bf16[2,176,512]{2,1,0:T(8,128)(2,1)S(1)}, bf16[2,176,512]{2,1,0:T(8,128)(2,1)S(1)}, u32[]{:S(2)}, u32[]{:S(2)}) collective-permute-start(bf16[2,176,512]{2,1,0:T(8,128)(2,1)S(1)} %get-tuple-element.89), channel_id=1, source_target_pairs={{0,12},{1,13},{2,14},{3,15},{4,0},{5,1},{6,2},{7,3},{8,4},{9,5},{1... | collective-permute-start | bytes 1081352 | tf_op jit(solution)/shard_map/ppermute | solution.py:42
  106.5 7.6 %experts.2 = (bf16[2,176,512]{2,1,0:T(8,128)(2,1)S(1)}, bf16[2,176,512]{2,1,0:T(8,128)(2,1)S(1)}, bf16[2,176,512]{2,1,0:T(8,128)(2,1)S(1)}, bf16[2,176,512]{2,1,...) custom-call(bf16[4,40,1024]{2,1,0:T(8,128)(2,1)S(1)} %get-tuple-elem, ...), custom_call_target="tpu_custom_call" | custom-call | tf_op jit(solution)/shard_map/experts/pallas_call | solution.py:208
  114.1 3.5 %collective-permute-start.30 = (bf16[2,4,40,512]{3,2,1,0:T(8,128)(2,1)S(1)}, bf16[2,4,40,512]{3,2,1,0:T(8,128)(2,1)S(1)}, u32[]{:S(2)}, u32[]{:S(2)}) collective-permute-start(bf16[2,4,40,512]{3,2,1,0:T(8,128)(2,1)S(1)} %get-tuple-element.96), channel_id=1, source_target_pairs={{0,3},{1,0},{2,1},{3,2},{4,7},{5,4},{6,5},{7,6},{8,11},{9,8},{10,9... | collective-permute-start | bytes 983048 | tf_op jit(solution)/shard_map/ppermute | solution.py:42
  117.7 3.8 %collective-permute-start.34 = (bf16[2,4,40,512]{3,2,1,0:T(8,128)(2,1)S(1)}, bf16[2,4,40,512]{3,2,1,0:T(8,128)(2,1)S(1)}, u32[]{:S(2)}, u32[]{:S(2)}) collective-permute-start(bf16[2,4,40,512]{3,2,1,0:T(8,128)(2,1)S(1)} %get-tuple-element.100), channel_id=1, source_target_pairs={{0,1},{1,2},{2,3},{3,0},{4,5},{5,6},{6,7},{7,4},{8,9},{9,10},{10,1... | collective-permute-start | bytes 983048 | tf_op jit(solution)/shard_map/ppermute | solution.py:42
  127.5 4.2 %collective-permute-start.29 = (bf16[2,176,512]{2,1,0:T(8,128)(2,1)S(1)}, bf16[2,176,512]{2,1,0:T(8,128)(2,1)S(1)}, u32[]{:S(2)}, u32[]{:S(2)}) collective-permute-start(bf16[2,176,512]{2,1,0:T(8,128)(2,1)S(1)} %get-tuple-element.93), channel_id=1, source_target_pairs={{0,4},{1,5},{2,6},{3,7},{4,8},{5,9},{6,10},{7,11},{8,12},{9,13},{1... | collective-permute-start | bytes 1081352 | tf_op jit(solution)/shard_map/ppermute | solution.py:42
  131.8 6.5 %collective-permute-start.24 = (bf16[2,176,512]{2,1,0:T(8,128)(2,1)S(1)}, bf16[2,176,512]{2,1,0:T(8,128)(2,1)S(1)}, u32[]{:S(2)}, u32[]{:S(2)}) collective-permute-start(bf16[2,176,512]{2,1,0:T(8,128)(2,1)S(1)} %get-tuple-element.88), channel_id=1, source_target_pairs={{0,12},{1,13},{2,14},{3,15},{4,0},{5,1},{6,2},{7,3},{8,4},{9,5},{1... | collective-permute-start | bytes 1081352 | tf_op jit(solution)/shard_map/ppermute | solution.py:42
  140.2 5.8 %collective-permute-start.28 = (bf16[2,176,512]{2,1,0:T(8,128)(2,1)S(1)}, bf16[2,176,512]{2,1,0:T(8,128)(2,1)S(1)}, u32[]{:S(2)}, u32[]{:S(2)}) collective-permute-start(bf16[2,176,512]{2,1,0:T(8,128)(2,1)S(1)} %get-tuple-element.92), channel_id=1, source_target_pairs={{0,4},{1,5},{2,6},{3,7},{4,8},{5,9},{6,10},{7,11},{8,12},{9,13},{1... | collective-permute-start | bytes 1081352 | tf_op jit(solution)/shard_map/ppermute | solution.py:42
  149.3 4.3 %collective-permute-done.26.refs_7_ = bf16[2,176,512]{2,1,0:T(8,128)(2,1)S(1)} collective-permute-done((bf16[2,176,512]{2,1,0:T(8,128)(2,1)S(1)}, bf16[2,176,512]{2,1,0:T(8,128)(2,1)S(1)}, u32[]{:S(2)}, u32[]{:S(2)}) %collective-permute-start.26) | collective-permute-done | bytes 360480 | tf_op jit(solution)/shard_map/ppermute | solution.py:42
  153.6 8.2 %collective-permute-done.28.refs_9_ = bf16[2,176,512]{2,1,0:T(8,128)(2,1)S(1)} collective-permute-done((bf16[2,176,512]{2,1,0:T(8,128)(2,1)S(1)}, bf16[2,176,512]{2,1,0:T(8,128)(2,1)S(1)}, u32[]{:S(2)}, u32[]{:S(2)}) %collective-permute-start.28) | collective-permute-done | bytes 360480 | tf_op jit(solution)/shard_map/ppermute | solution.py:42
  163.8 4.9 %collective-permute-start.36 = (bf16[264,512]{1,0:T(8,128)(2,1)S(1)}, bf16[264,512]{1,0:T(8,128)(2,1)S(1)}, u32[]{:S(2)}, u32[]{:S(2)}) collective-permute-start(bf16[264,512]{1,0:T(8,128)(2,1)S(1)} %get-tuple-element.103), channel_id=1, source_target_pairs={{0,3},{1,0},{2,1},{3,2},{4,7},{5,4},{6,5},{7,6},{8,11},{9,8},{10,9... | collective-permute-start | bytes 811016 | tf_op jit(solution)/shard_map/ppermute | solution.py:42
  170.7 5.8 %collective-permute-done.40.refs_6_ = bf16[256,512]{1,0:T(8,128)(2,1)S(1)} collective-permute-done((bf16[256,512]{1,0:T(8,128)(2,1)S(1)}, bf16[256,512]{1,0:T(8,128)(2,1)S(1)}, u32[]{:S(2)}, u32[]{:S(2)}) %collective-permute-start.40) | collective-permute-done | bytes 262176 | tf_op jit(solution)/shard_map/ppermute | solution.py:42
  176.5 7.9 %collective-permute-done.41.refs_7_ = bf16[256,512]{1,0:T(8,128)(2,1)S(1)} collective-permute-done((bf16[256,512]{1,0:T(8,128)(2,1)S(1)}, bf16[256,512]{1,0:T(8,128)(2,1)S(1)}, u32[]{:S(2)}, u32[]{:S(2)}) %collective-permute-start.41) | collective-permute-done | bytes 262176 | tf_op jit(solution)/shard_map/ppermute | solution.py:42
  187.7 6.4 %weight_grads.2 = (bf16[4,1024,384]{2,1,0:T(8,128)(2,1)}, bf16[4,1024,384]{2,1,0:T(8,128)(2,1)}) custom-call(s32[64]{0:T(128)S(1)} %reshape_squeeze.3.count_ref, bf16[4,640,1024]{2,1,0:T(8,128)(2,1)} %bitcast.58, bf16[4,640,384]{2,1,0:T(8,128)(2,1)} %bitcast.60, bf16[4,640,384]{2,1,0:T(8,128)(2,1)} %bitcast.62), custom_call_target="tpu_custom_call" | custom-call | tf_op jit(solution)/shard_map/weight_grads/pallas_call | solution.py:333
  194.2 6.4 %weight_grads.3 = (bf16[4,1024,384]{2,1,0:T(8,128)(2,1)}, bf16[4,1024,384]{2,1,0:T(8,128)(2,1)}) custom-call(s32[64]{0:T(128)S(1)} %reshape_squeeze.3.count_ref, bf16[4,640,1024]{2,1,0:T(8,128)(2,1)} %bitcast.59, bf16[4,640,384]{2,1,0:T(8,128)(2,1)} %bitcast.61, bf16[4,640,384]{2,1,0:T(8,128)(2,1)} %bitcast.63, ...), custom_call_target="tpu_custom_call", output_to_operand_aliasing={{0}: (4, {}), {1}: (5, {})} | custom-call | tf_op jit(solution)/shard_map/weight_grads/pallas_call | solution.py:333
  (97 shorter events, 65.1 us)
Async XLA Ops:
  3.8 26.3 %collective-permute-start.5 = (bf16[264,1024]{1,0:T(8,128)(2,1)}, bf16[264,1024]{1,0:T(8,128)(2,1)S(1)}, u32[]{:S(2)}, u32[]{:S(2)}) collective-permute-start(bf16[264,1024]{1,0:T(8,128)(2,1)} %get-tuple-element.114.refs_4_.refs_1_), channel_id=1, source_target_pairs={{0,12},{1,13},{2,14},{3,15},{4,0},{5,1},{6,2},{7,3},{8,4},{9,5},{1... | collective-permute-start | bytes 1622024 | tf_op jit(solution)/shard_map/ppermute | solution.py:42
  7.4 26.0 %collective-permute-start.4 = (bf16[264,1024]{1,0:T(8,128)(2,1)}, bf16[264,1024]{1,0:T(8,128)(2,1)}, u32[]{:S(2)}, u32[]{:S(2)}) collective-permute-start(bf16[264,1024]{1,0:T(8,128)(2,1)} %get-tuple-element.114.refs_4_.refs_1_), channel_id=1, source_target_pairs={{0,8},{1,9},{2,10},{3,11},{4,12},{5,13},{6,14},{7,15},{8,0},{9,1},... | collective-permute-start | bytes 1622024 | tf_op jit(solution)/shard_map/ppermute | solution.py:42
  7.7 27.3 %collective-permute-start.3 = (bf16[264,1024]{1,0:T(8,128)(2,1)}, bf16[264,1024]{1,0:T(8,128)(2,1)}, u32[]{:S(2)}, u32[]{:S(2)}) collective-permute-start(bf16[264,1024]{1,0:T(8,128)(2,1)} %get-tuple-element.114.refs_4_.refs_1_), channel_id=1, source_target_pairs={{0,4},{1,5},{2,6},{3,7},{4,8},{5,9},{6,10},{7,11},{8,12},{9,13},{1... | collective-permute-start | bytes 1622024 | tf_op jit(solution)/shard_map/ppermute | solution.py:42
  8.4 31.3 %collective-permute-start.2 = (bf16[264,1024]{1,0:T(8,128)(2,1)}, bf16[264,1024]{1,0:T(8,128)(2,1)}, u32[]{:S(2)}, u32[]{:S(2)}) collective-permute-start(bf16[264,1024]{1,0:T(8,128)(2,1)} %get-tuple-element.115.refs_0_.meta), channel_id=1, source_target_pairs={{0,3},{1,0},{2,1},{3,2},{4,7},{5,4},{6,5},{7,6},{8,11},{9,8},{10,9... | collective-permute-start | bytes 1622024 | tf_op jit(solution)/shard_map/ppermute | solution.py:42
  12.2 27.5 %collective-permute-start.1 = (bf16[264,1024]{1,0:T(8,128)(2,1)}, bf16[264,1024]{1,0:T(8,128)(2,1)}, u32[]{:S(2)}, u32[]{:S(2)}) collective-permute-start(bf16[264,1024]{1,0:T(8,128)(2,1)} %get-tuple-element.115.refs_0_.meta), channel_id=1, source_target_pairs={{0,2},{1,3},{2,0},{3,1},{4,6},{5,7},{6,4},{7,5},{8,10},{9,11},{10,... | collective-permute-start | bytes 1622024 | tf_op jit(solution)/shard_map/ppermute | solution.py:42
  35.0 17.7 %collective-permute-start.7 = (bf16[4,40,1024]{2,1,0:T(8,128)(2,1)S(1)}, bf16[4,40,1024]{2,1,0:T(8,128)(2,1)S(1)}, u32[]{:S(2)}, u32[]{:S(2)}) collective-permute-start(bf16[4,40,1024]{2,1,0:T(8,128)(2,1)S(1)} %get-tuple-element.64), channel_id=1, source_target_pairs={{0,8},{1,9},{2,10},{3,11},{4,12},{5,13},{6,14},{7,15},{8,0},{9,1},... | collective-permute-start | bytes 983048 | tf_op jit(solution)/shard_map/ppermute | solution.py:42
  48.0 19.4 %collective-permute-start.18 = (bf16[2,3,40,1024]{3,2,1,0:T(8,128)(2,1)S(1)}, bf16[2,3,40,1024]{3,2,1,0:T(8,128)(2,1)S(1)}, u32[]{:S(2)}, u32[]{:S(2)}) collective-permute-start(bf16[2,3,40,1024]{3,2,1,0:T(8,128)(2,1)S(1)} %get-tuple-element.80), channel_id=1, source_target_pairs={{0,4},{1,5},{2,6},{3,7},{4,8},{5,9},{6,10},{7,11},{8,12},{9,13},{1... | collective-permute-start | bytes 1474568 | tf_op jit(solution)/shard_map/ppermute | solution.py:42
  52.7 20.6 %collective-permute-start.19 = (bf16[2,3,40,1024]{3,2,1,0:T(8,128)(2,1)S(1)}, bf16[2,3,40,1024]{3,2,1,0:T(8,128)(2,1)S(1)}, u32[]{:S(2)}, u32[]{:S(2)}) collective-permute-start(bf16[2,3,40,1024]{3,2,1,0:T(8,128)(2,1)S(1)} %get-tuple-element.81), channel_id=1, source_target_pairs={{0,8},{1,9},{2,10},{3,11},{4,12},{5,13},{6,14},{7,15},{8,0},{9,1},... | collective-permute-start | bytes 1474568 | tf_op jit(solution)/shard_map/ppermute | solution.py:42
  56.5 19.6 %collective-permute-start.20 = (bf16[2,3,40,1024]{3,2,1,0:T(8,128)(2,1)S(1)}, bf16[2,3,40,1024]{3,2,1,0:T(8,128)(2,1)S(1)}, u32[]{:S(2)}, u32[]{:S(2)}) collective-permute-start(bf16[2,3,40,1024]{3,2,1,0:T(8,128)(2,1)S(1)} %get-tuple-element.82), channel_id=1, source_target_pairs={{0,12},{1,13},{2,14},{3,15},{4,0},{5,1},{6,2},{7,3},{8,4},{9,5},{1... | collective-permute-start | bytes 1474568 | tf_op jit(solution)/shard_map/ppermute | solution.py:42
  67.5 17.8 %collective-permute-start.23 = (bf16[2,3,40,1024]{3,2,1,0:T(8,128)(2,1)S(1)}, bf16[2,3,40,1024]{3,2,1,0:T(8,128)(2,1)S(1)}, u32[]{:S(2)}, u32[]{:S(2)}) collective-permute-start(bf16[2,3,40,1024]{3,2,1,0:T(8,128)(2,1)S(1)} %get-tuple-element.86), channel_id=1, source_target_pairs={{0,3},{1,0},{2,1},{3,2},{4,7},{5,4},{6,5},{7,6},{8,11},{9,8},{10,9... | collective-permute-start | bytes 1474568 | tf_op jit(solution)/shard_map/ppermute | solution.py:42
  76.1 21.0 %collective-permute-start.10 = (bf16[2,3,40,1024]{3,2,1,0:T(8,128)(2,1)S(1)}, bf16[2,3,40,1024]{3,2,1,0:T(8,128)(2,1)S(1)}, u32[]{:S(2)}, u32[]{:S(2)}) collective-permute-start(bf16[2,3,40,1024]{3,2,1,0:T(8,128)(2,1)S(1)} %get-tuple-element.68), channel_id=1, source_target_pairs={{0,8},{1,9},{2,10},{3,11},{4,12},{5,13},{6,14},{7,15},{8,0},{9,1},... | collective-permute-start | bytes 1474568 | tf_op jit(solution)/shard_map/ppermute | solution.py:42
  76.5 21.4 %collective-permute-start.11 = (bf16[2,3,40,1024]{3,2,1,0:T(8,128)(2,1)S(1)}, bf16[2,3,40,1024]{3,2,1,0:T(8,128)(2,1)S(1)}, u32[]{:S(2)}, u32[]{:S(2)}) collective-permute-start(bf16[2,3,40,1024]{3,2,1,0:T(8,128)(2,1)S(1)} %get-tuple-element.69), channel_id=1, source_target_pairs={{0,12},{1,13},{2,14},{3,15},{4,0},{5,1},{6,2},{7,3},{8,4},{9,5},{1... | collective-permute-start | bytes 1474568 | tf_op jit(solution)/shard_map/ppermute | solution.py:42
  79.5 21.9 %collective-permute-start.15 = (bf16[2,3,40,1024]{3,2,1,0:T(8,128)(2,1)S(1)}, bf16[2,3,40,1024]{3,2,1,0:T(8,128)(2,1)S(1)}, u32[]{:S(2)}, u32[]{:S(2)}) collective-permute-start(bf16[2,3,40,1024]{3,2,1,0:T(8,128)(2,1)S(1)} %get-tuple-element.75), channel_id=1, source_target_pairs={{0,1},{1,2},{2,3},{3,0},{4,5},{5,6},{6,7},{7,4},{8,9},{9,10},{10,1... | collective-permute-start | bytes 1474568 | tf_op jit(solution)/shard_map/ppermute | solution.py:42
  85.3 20.0 %collective-permute-start.16 = (bf16[2,3,40,1024]{3,2,1,0:T(8,128)(2,1)S(1)}, bf16[2,3,40,1024]{3,2,1,0:T(8,128)(2,1)S(1)}, u32[]{:S(2)}, u32[]{:S(2)}) collective-permute-start(bf16[2,3,40,1024]{3,2,1,0:T(8,128)(2,1)S(1)} %get-tuple-element.76), channel_id=1, source_target_pairs={{0,2},{1,3},{2,0},{3,1},{4,6},{5,7},{6,4},{7,5},{8,10},{9,11},{10,... | collective-permute-start | bytes 1474568 | tf_op jit(solution)/shard_map/ppermute | solution.py:42
  86.6 19.9 %collective-permute-start.17 = (bf16[2,3,40,1024]{3,2,1,0:T(8,128)(2,1)S(1)}, bf16[2,3,40,1024]{3,2,1,0:T(8,128)(2,1)S(1)}, u32[]{:S(2)}, u32[]{:S(2)}) collective-permute-start(bf16[2,3,40,1024]{3,2,1,0:T(8,128)(2,1)S(1)} %get-tuple-element.77), channel_id=1, source_target_pairs={{0,3},{1,0},{2,1},{3,2},{4,7},{5,4},{6,5},{7,6},{8,11},{9,8},{10,9... | collective-permute-start | bytes 1474568 | tf_op jit(solution)/shard_map/ppermute | solution.py:42
  97.1 20.5 %collective-permute-start.31 = (bf16[2,4,40,512]{3,2,1,0:T(8,128)(2,1)S(1)}, bf16[2,4,40,512]{3,2,1,0:T(8,128)(2,1)S(1)}, u32[]{:S(2)}, u32[]{:S(2)}) collective-permute-start(bf16[2,4,40,512]{3,2,1,0:T(8,128)(2,1)S(1)} %get-tuple-element.97), channel_id=1, source_target_pairs={{0,3},{1,0},{2,1},{3,2},{4,7},{5,4},{6,5},{7,6},{8,11},{9,8},{10,9... | collective-permute-start | bytes 983048 | tf_op jit(solution)/shard_map/ppermute | solution.py:42
  97.9 19.8 %collective-permute-start.33 = (bf16[2,4,40,512]{3,2,1,0:T(8,128)(2,1)S(1)}, bf16[2,4,40,512]{3,2,1,0:T(8,128)(2,1)S(1)}, u32[]{:S(2)}, u32[]{:S(2)}) collective-permute-start(bf16[2,4,40,512]{3,2,1,0:T(8,128)(2,1)S(1)} %get-tuple-element.99), channel_id=1, source_target_pairs={{0,2},{1,3},{2,0},{3,1},{4,6},{5,7},{6,4},{7,5},{8,10},{9,11},{10,... | collective-permute-start | bytes 983048 | tf_op jit(solution)/shard_map/ppermute | solution.py:42
  101.4 38.9 %collective-permute-start.25 = (bf16[2,176,512]{2,1,0:T(8,128)(2,1)S(1)}, bf16[2,176,512]{2,1,0:T(8,128)(2,1)S(1)}, u32[]{:S(2)}, u32[]{:S(2)}) collective-permute-start(bf16[2,176,512]{2,1,0:T(8,128)(2,1)S(1)} %get-tuple-element.89), channel_id=1, source_target_pairs={{0,12},{1,13},{2,14},{3,15},{4,0},{5,1},{6,2},{7,3},{8,4},{9,5},{1... | collective-permute-start | bytes 1081352 | tf_op jit(solution)/shard_map/ppermute | solution.py:42
  117.7 20.7 %collective-permute-start.34 = (bf16[2,4,40,512]{3,2,1,0:T(8,128)(2,1)S(1)}, bf16[2,4,40,512]{3,2,1,0:T(8,128)(2,1)S(1)}, u32[]{:S(2)}, u32[]{:S(2)}) collective-permute-start(bf16[2,4,40,512]{3,2,1,0:T(8,128)(2,1)S(1)} %get-tuple-element.100), channel_id=1, source_target_pairs={{0,1},{1,2},{2,3},{3,0},{4,5},{5,6},{6,7},{7,4},{8,9},{9,10},{10,1... | collective-permute-start | bytes 983048 | tf_op jit(solution)/shard_map/ppermute | solution.py:42
  121.5 27.7 %collective-permute-start.27 = (bf16[2,176,512]{2,1,0:T(8,128)(2,1)S(1)}, bf16[2,176,512]{2,1,0:T(8,128)(2,1)S(1)}, u32[]{:S(2)}, u32[]{:S(2)}) collective-permute-start(bf16[2,176,512]{2,1,0:T(8,128)(2,1)S(1)} %get-tuple-element.91), channel_id=1, source_target_pairs={{0,8},{1,9},{2,10},{3,11},{4,12},{5,13},{6,14},{7,15},{8,0},{9,1},... | collective-permute-start | bytes 1081352 | tf_op jit(solution)/shard_map/ppermute | solution.py:42
  127.5 21.7 %collective-permute-start.29 = (bf16[2,176,512]{2,1,0:T(8,128)(2,1)S(1)}, bf16[2,176,512]{2,1,0:T(8,128)(2,1)S(1)}, u32[]{:S(2)}, u32[]{:S(2)}) collective-permute-start(bf16[2,176,512]{2,1,0:T(8,128)(2,1)S(1)} %get-tuple-element.93), channel_id=1, source_target_pairs={{0,4},{1,5},{2,6},{3,7},{4,8},{5,9},{6,10},{7,11},{8,12},{9,13},{1... | collective-permute-start | bytes 1081352 | tf_op jit(solution)/shard_map/ppermute | solution.py:42
  140.2 21.6 %collective-permute-start.28 = (bf16[2,176,512]{2,1,0:T(8,128)(2,1)S(1)}, bf16[2,176,512]{2,1,0:T(8,128)(2,1)S(1)}, u32[]{:S(2)}, u32[]{:S(2)}) collective-permute-start(bf16[2,176,512]{2,1,0:T(8,128)(2,1)S(1)} %get-tuple-element.92), channel_id=1, source_target_pairs={{0,4},{1,5},{2,6},{3,7},{4,8},{5,9},{6,10},{7,11},{8,12},{9,13},{1... | collective-permute-start | bytes 1081352 | tf_op jit(solution)/shard_map/ppermute | solution.py:42
  163.8 20.6 %collective-permute-start.36 = (bf16[264,512]{1,0:T(8,128)(2,1)S(1)}, bf16[264,512]{1,0:T(8,128)(2,1)S(1)}, u32[]{:S(2)}, u32[]{:S(2)}) collective-permute-start(bf16[264,512]{1,0:T(8,128)(2,1)S(1)} %get-tuple-element.103), channel_id=1, source_target_pairs={{0,3},{1,0},{2,1},{3,2},{4,7},{5,4},{6,5},{7,6},{8,11},{9,8},{10,9... | collective-permute-start | bytes 811016 | tf_op jit(solution)/shard_map/ppermute | solution.py:42
  184.7 17.6 %collective-permute-start.42 = (bf16[1,256,1024]{2,1,0:T(8,128)(2,1)S(1)}, bf16[1,256,1024]{2,1,0:T(8,128)(2,1)S(1)}, u32[]{:S(2)}, u32[]{:S(2)}) collective-permute-start(bf16[1,256,1024]{2,1,0:T(8,128)(2,1)S(1)} %finish.1), channel_id=1, source_target_pairs={{16,0},{32,16},{48,32},{64,48},{80,64},{96,80},{112,96},{17,1},{33... | collective-permute-start | bytes 1572872 | tf_op jit(solution)/shard_map/ppermute | solution.py:411
  (26 other events, 470.1 us)

commit v2 on v1

--- a/solution.py
+++ b/solution.py
@@ -182,16 +182,14 @@
     prob = jnp.sum(hidden * hg, axis=1, keepdims=True)
     gate_grad = (hg * up * sigma * (1.0 + gate * (1.0 - sigma))).astype(BF)
     up_grad = (hg * active).astype(BF)
-    lane = iota((CAP, 128), 1)
+    lane = iota((8, 128), 1)
     for i in range(4):
-        mine = jnp.zeros((CAP, 128), F32)
-        for j in range(4):
-            at = (4 * i + j) * CAP
-            mine = jnp.where(lane == j, prob[at : at + CAP], mine)
+        tiles = [jnp.zeros((8, 128), F32) for _ in range(4)]
         for t in range(5):
-            a_outs[i][e, 160 + 8 * (t // 4) : 168 + 8 * (t // 4), 128 * (t % 4) : 128 * (t % 4) + 128] = mine[
-                8 * t : 8 * t + 8
-            ].astype(BF)
+            for j in range(4):
+                at = (4 * i + j) * CAP + 8 * t
+                tiles[t % 4] = jnp.where(lane == j + 4 * (t // 4), prob[at : at + 8], tiles[t % 4])
+        a_outs[i][e, 160:168, :] = jnp.concatenate(tiles, axis=1).astype(BF)
     back = lax.dot_general(gate_grad, wg, nt, preferred_element_type=F32)
     back = back + lax.dot_general(up_grad, wu, nt, preferred_element_type=F32)
     for i in range(4):
@@ -207,7 +205,7 @@
     xs, gs = ([a.reshape(2, 120, 1024) for a in part] for part in (xs, gs))
     outs = pl.pallas_call(
         functools.partial(expert_body, half=half),
-        out_shape=(pltpu.VMEM((2, 176, 512), BF),) * 4 + (pltpu.VMEM((2, SIDE, CAP, 512), BF),) * 4,
+        out_shape=(pltpu.VMEM((2, 168, 512), BF),) * 4 + (pltpu.VMEM((2, SIDE, CAP, 512), BF),) * 4,
         grid=(2,),
         in_specs=[VMEM_SPEC] * 16 + [w_in, w_in, w_out],
         out_specs=[VMEM_SPEC] * 8,
@@ -217,51 +215,47 @@
     return outs[0:4], outs[4:8]
 
 
-def values_at_tokens(rank, columns, j):
+def values_at_tokens(rank, tails, j):
     slot = iota((CAP, 256), 0).astype(F32)
     found = []
     for r in range(16):
-        one = jnp.where(rank[r : r + 1] == slot, columns[r][:, j : j + 1], 0.0)
+        lanes = [128 * (t % 4) + j + 4 * (t // 4) for t in range(5)]
+        column = jnp.concatenate([tails[r][:, n : n + 1] for n in lanes], axis=0)
+        one = jnp.where(rank[r : r + 1] == slot, column, 0.0)
         found.append(jnp.sum(one, axis=0, keepdims=True))
     return jnp.concatenate(found, axis=0)
 
 
-def combine_body(*refs):
-    rank_ref, weights, rows_in, outs = refs[0], refs[1:3], refs[3:19], refs[19:27]
-    columns = []
-    for source in rows_in[0:8]:
-        for e in range(2):
-            tile = [
-                source[e, 160 + 8 * (t // 4) : 168 + 8 * (t // 4), 128 * (t % 4) : 128 * (t % 4) + 128]
-                for t in range(5)
-            ]
-            columns.append(jnp.concatenate([t.astype(F32) for t in tile], axis=0))
-    for j in range(4):
+def combine_body(*refs, sources):
+    rank_ref, weights, rows_in, outs = refs[0], refs[1:3], refs[3:19], refs[19:]
+    tails = [source[e, 160:168, :].astype(F32) for source in rows_in[0:8] for e in range(2)]
+    for at, j in enumerate(sources):
         for c in range(2):
             pieces = []
             for source in rows_in[8 * c : 8 * c + 8]:
                 for e in range(2):
                     pieces.append(source[e, CAP * j : CAP * j + CAP] if c == 0 else source[e, j])
             joined = jnp.concatenate([p.astype(F32) for p in pieces], axis=0).astype(BF)
-            out = outs[4 * c + j]
+            out = outs[len(sources) * c + at]
             out[0:256, :] = jnp.dot(weights[c][j], joined, preferred_element_type=F32).astype(BF)
             if c == 0:
-                values = values_at_tokens(rank_ref[j], columns, j)
+                values = values_at_tokens(rank_ref[j], tails, j)
                 out[256:264, 0:256] = values[0:8].astype(BF)
                 out[256:264, 256:512] = values[8:16].astype(BF)
 
 
-def combine(ranks, spread_a, spread_b, lows, highs):
+def combine(ranks, spread_a, spread_b, lows, highs, sources):
     both = [pair[half][i] for pair in (lows, highs) for i in range(4) for half in range(2)]
+    count = len(sources)
     outs = pl.pallas_call(
-        combine_body,
-        out_shape=(pltpu.VMEM((264, 512), BF),) * 4 + (pltpu.VMEM((256, 512), BF),) * 4,
+        functools.partial(combine_body, sources=sources),
+        out_shape=(pltpu.VMEM((264, 512), BF),) * count + (pltpu.VMEM((256, 512), BF),) * count,
         in_specs=[VMEM_SPEC] * 19,
-        out_specs=[VMEM_SPEC] * 8,
+        out_specs=[VMEM_SPEC] * (2 * count),
         compiler_params=room(12),
         name="combine",
     )(*in_vmem([ranks, spread_a, spread_b, *both]))
-    return outs[0:4], outs[4:8]
+    return dict(zip(sources, outs[:count])), dict(zip(sources, outs[count:]))
 
 
 def pick_probs_body(place_ref, meta, *refs):
@@ -404,7 +398,9 @@
         lows.append(spread_out(back_a, along_y, -1))
         highs.append(spread_out(back_b, along_z, -1))
     spread_a, spread_b, ranks = spreads(dest, blocks_a, blocks_b)
-    made_a, made_b = combine(ranks, spread_a, spread_b, lows, highs)
+    made_a, made_b = combine(ranks, spread_a, spread_b, lows, highs, (2,))
+    more_a, more_b = combine(ranks, spread_a, spread_b, lows, highs, (1, 3, 0))
+    made_a, made_b = {**made_a, **more_a}, {**made_b, **more_b}
     left = spread_out(made_a, along_z, -1)
     right = spread_out(made_b, along_y, -1)
     input_grad = finish(left, right)

time: 203 us -> 199 us (0.980)
  waiting for transfers between devices: 71.5 us -> 65.3 us
    ppermute x42, waiting for transfers between devices: 71.5 us -> 65.3 us  [moved(): return lax.ppermute(array, 'ep', pairs)]
  transfers between devices with their start and end apart: 43 -> 43, of which waited for: 15 -> 16; matrix products, arithmetic and copies ran while one was open for 0% -> 0% of each run, Pallas kernels for 21% -> 22%
where the time goes in v2:
time: 199 us
  starting transfers between devices  82.6 us (42%)
  waiting for transfers between devices  65.3 us (33%)
  Pallas kernels  43.9 us (22%)
  other arithmetic  3.37 us (2%)
  local copies, waits for them, and re-layouts  2.83 us (1%)
    ppermute x42, starting transfers between devices, moved(): return lax.ppermute(array, 'ep', pairs)  79.1 us
    ppermute x42, waiting for transfers between devices, moved(): return lax.ppermute(array, 'ep', pairs)  65.3 us
    pallas_call x2, Pallas kernels, experts(): pl.pallas_call(functools.partial(expert_body, half=half), out_shape=(pltp...  15.3 us
    pallas_call x2, Pallas kernels, weight_grads(): pl.pallas_call(functools.partial(weight_grads_body, first=first), out_sha...  12.9 us
    pallas_call x2, Pallas kernels, select(): pl.pallas_call(functools.partial(select_body, first=first), out_shape=(pl...  6.18 us
  transfers between devices with their start and end apart: 43, of which 16 were waited for; matrix products, arithmetic and copies ran while one was open for 0% of the time, Pallas kernels for 22%

profile of v2, /device:TPU:1, one launch (start us, length us, event | category | flops | bytes accessed | tf_op | source)
XLA Modules:
  0.0 198.9 jit_solution(15161257988268046703)
XLA Ops:
  3.8 3.6 %collective-permute-start.5 = (bf16[264,1024]{1,0:T(8,128)(2,1)}, bf16[264,1024]{1,0:T(8,128)(2,1)S(1)}, u32[]{:S(2)}, u32[]{:S(2)}) collective-permute-start(bf16[264,1024]{1,0:T(8,128)(2,1)} %get-tuple-element.114.refs_4_.refs_1_), channel_id=1, source_target_pairs={{0,12},{1,13},{2,14},{3,15},{4,0},{5,1},{6,2},{7,3},{8,4},{9,5},{1... | collective-permute-start | bytes 1622024 | tf_op jit(solution)/shard_map/ppermute | solution.py:42
  8.4 3.8 %collective-permute-start.2 = (bf16[264,1024]{1,0:T(8,128)(2,1)}, bf16[264,1024]{1,0:T(8,128)(2,1)}, u32[]{:S(2)}, u32[]{:S(2)}) collective-permute-start(bf16[264,1024]{1,0:T(8,128)(2,1)} %get-tuple-element.115.refs_0_.meta), channel_id=1, source_target_pairs={{0,3},{1,0},{2,1},{3,2},{4,7},{5,4},{6,5},{7,6},{8,11},{9,8},{10,9... | collective-permute-start | bytes 1622024 | tf_op jit(solution)/shard_map/ppermute | solution.py:42
  12.2 17.9 %collective-permute-done.5.refs_7_.refs_5_ = bf16[264,1024]{1,0:T(8,128)(2,1)S(1)} collective-permute-done((bf16[264,1024]{1,0:T(8,128)(2,1)}, bf16[264,1024]{1,0:T(8,128)(2,1)S(1)}, u32[]{:S(2)}, u32[]{:S(2)}) %collective-permute-start.5) | collective-permute-done | bytes 540704 | tf_op jit(solution)/shard_map/ppermute | solution.py:42
  35.0 4.7 %collective-permute-start.7 = (bf16[4,40,1024]{2,1,0:T(8,128)(2,1)S(1)}, bf16[4,40,1024]{2,1,0:T(8,128)(2,1)S(1)}, u32[]{:S(2)}, u32[]{:S(2)}) collective-permute-start(bf16[4,40,1024]{2,1,0:T(8,128)(2,1)S(1)} %get-tuple-element.64), channel_id=1, source_target_pairs={{0,8},{1,9},{2,10},{3,11},{4,12},{5,13},{6,14},{7,15},{8,0},{9,1},... | collective-permute-start | bytes 983048 | tf_op jit(solution)/shard_map/ppermute | solution.py:42
  49.0 3.7 %collective-permute-done.7.refs_2_ = bf16[4,40,1024]{2,1,0:T(8,128)(2,1)S(1)} collective-permute-done((bf16[4,40,1024]{2,1,0:T(8,128)(2,1)S(1)}, bf16[4,40,1024]{2,1,0:T(8,128)(2,1)S(1)}, u32[]{:S(2)}, u32[]{:S(2)}) %collective-permute-start.7) | collective-permute-done | bytes 327712 | tf_op jit(solution)/shard_map/ppermute | solution.py:42
  68.7 4.5 %collective-permute-done.19 = bf16[2,3,40,1024]{3,2,1,0:T(8,128)(2,1)S(1)} collective-permute-done((bf16[2,3,40,1024]{3,2,1,0:T(8,128)(2,1)S(1)}, bf16[2,3,40,1024]{3,2,1,0:T(8,128)(2,1)S(1)}, u32[]{:S(2)}, u32[]{:S(2)}) %collective-permute-start.19) | collective-permute-done | bytes 491552 | tf_op jit(solution)/shard_map/ppermute | solution.py:42
  80.3 5.0 %collective-permute-done.23 = bf16[2,3,40,1024]{3,2,1,0:T(8,128)(2,1)S(1)} collective-permute-done((bf16[2,3,40,1024]{3,2,1,0:T(8,128)(2,1)S(1)}, bf16[2,3,40,1024]{3,2,1,0:T(8,128)(2,1)S(1)}, u32[]{:S(2)}, u32[]{:S(2)}) %collective-permute-start.23) | collective-permute-done | bytes 491552 | tf_op jit(solution)/shard_map/ppermute | solution.py:42
  89.4 7.7 %experts.3 = (bf16[2,168,512]{2,1,0:T(8,128)(2,1)S(1)}, bf16[2,168,512]{2,1,0:T(8,128)(2,1)S(1)}, bf16[2,168,512]{2,1,0:T(8,128)(2,1)S(1)}, bf16[2,168,512]{2,1,...) custom-call(bf16[4,40,1024]{2,1,0:T(8,128)(2,1)S(1)} %get-tuple-elem, ...), custom_call_target="tpu_custom_call" | custom-call | tf_op jit(solution)/shard_map/experts/pallas_call | solution.py:206
  97.9 3.5 %collective-permute-start.33 = (bf16[2,4,40,512]{3,2,1,0:T(8,128)(2,1)S(1)}, bf16[2,4,40,512]{3,2,1,0:T(8,128)(2,1)S(1)}, u32[]{:S(2)}, u32[]{:S(2)}) collective-permute-start(bf16[2,4,40,512]{3,2,1,0:T(8,128)(2,1)S(1)} %get-tuple-element.99), channel_id=1, source_target_pairs={{0,2},{1,3},{2,0},{3,1},{4,6},{5,7},{6,4},{7,5},{8,10},{9,11},{10,... | collective-permute-start | bytes 983048 | tf_op jit(solution)/shard_map/ppermute | solution.py:42
  101.4 4.0 %collective-permute-start.25 = (bf16[2,168,512]{2,1,0:T(8,128)(2,1)S(1)}, bf16[2,168,512]{2,1,0:T(8,128)(2,1)S(1)}, u32[]{:S(2)}, u32[]{:S(2)}) collective-permute-start(bf16[2,168,512]{2,1,0:T(8,128)(2,1)S(1)} %get-tuple-element.89), channel_id=1, source_target_pairs={{0,12},{1,13},{2,14},{3,15},{4,0},{5,1},{6,2},{7,3},{8,4},{9,5},{1... | collective-permute-start | bytes 1032200 | tf_op jit(solution)/shard_map/ppermute | solution.py:42
  106.5 7.7 %experts.2 = (bf16[2,168,512]{2,1,0:T(8,128)(2,1)S(1)}, bf16[2,168,512]{2,1,0:T(8,128)(2,1)S(1)}, bf16[2,168,512]{2,1,0:T(8,128)(2,1)S(1)}, bf16[2,168,512]{2,1,...) custom-call(bf16[4,40,1024]{2,1,0:T(8,128)(2,1)S(1)} %get-tuple-elem, ...), custom_call_target="tpu_custom_call" | custom-call | tf_op jit(solution)/shard_map/experts/pallas_call | solution.py:206
  114.2 3.5 %collective-permute-start.30 = (bf16[2,4,40,512]{3,2,1,0:T(8,128)(2,1)S(1)}, bf16[2,4,40,512]{3,2,1,0:T(8,128)(2,1)S(1)}, u32[]{:S(2)}, u32[]{:S(2)}) collective-permute-start(bf16[2,4,40,512]{3,2,1,0:T(8,128)(2,1)S(1)} %get-tuple-element.96), channel_id=1, source_target_pairs={{0,3},{1,0},{2,1},{3,2},{4,7},{5,4},{6,5},{7,6},{8,11},{9,8},{10,9... | collective-permute-start | bytes 983048 | tf_op jit(solution)/shard_map/ppermute | solution.py:42
  117.7 3.8 %collective-permute-start.34 = (bf16[2,4,40,512]{3,2,1,0:T(8,128)(2,1)S(1)}, bf16[2,4,40,512]{3,2,1,0:T(8,128)(2,1)S(1)}, u32[]{:S(2)}, u32[]{:S(2)}) collective-permute-start(bf16[2,4,40,512]{3,2,1,0:T(8,128)(2,1)S(1)} %get-tuple-element.100), channel_id=1, source_target_pairs={{0,1},{1,2},{2,3},{3,0},{4,5},{5,6},{6,7},{7,4},{8,9},{9,10},{10,1... | collective-permute-start | bytes 983048 | tf_op jit(solution)/shard_map/ppermute | solution.py:42
  127.5 4.2 %collective-permute-start.29 = (bf16[2,168,512]{2,1,0:T(8,128)(2,1)S(1)}, bf16[2,168,512]{2,1,0:T(8,128)(2,1)S(1)}, u32[]{:S(2)}, u32[]{:S(2)}) collective-permute-start(bf16[2,168,512]{2,1,0:T(8,128)(2,1)S(1)} %get-tuple-element.93), channel_id=1, source_target_pairs={{0,4},{1,5},{2,6},{3,7},{4,8},{5,9},{6,10},{7,11},{8,12},{9,13},{1... | collective-permute-start | bytes 1032200 | tf_op jit(solution)/shard_map/ppermute | solution.py:42
  131.8 6.5 %collective-permute-start.24 = (bf16[2,168,512]{2,1,0:T(8,128)(2,1)S(1)}, bf16[2,168,512]{2,1,0:T(8,128)(2,1)S(1)}, u32[]{:S(2)}, u32[]{:S(2)}) collective-permute-start(bf16[2,168,512]{2,1,0:T(8,128)(2,1)S(1)} %get-tuple-element.88), channel_id=1, source_target_pairs={{0,12},{1,13},{2,14},{3,15},{4,0},{5,1},{6,2},{7,3},{8,4},{9,5},{1... | collective-permute-start | bytes 1032200 | tf_op jit(solution)/shard_map/ppermute | solution.py:42
  140.3 5.7 %collective-permute-start.28 = (bf16[2,168,512]{2,1,0:T(8,128)(2,1)S(1)}, bf16[2,168,512]{2,1,0:T(8,128)(2,1)S(1)}, u32[]{:S(2)}, u32[]{:S(2)}) collective-permute-start(bf16[2,168,512]{2,1,0:T(8,128)(2,1)S(1)} %get-tuple-element.92), channel_id=1, source_target_pairs={{0,4},{1,5},{2,6},{3,7},{4,8},{5,9},{6,10},{7,11},{8,12},{9,13},{1... | collective-permute-start | bytes 1032200 | tf_op jit(solution)/shard_map/ppermute | solution.py:42
  149.3 3.6 %collective-permute-done.26.refs_7_ = bf16[2,168,512]{2,1,0:T(8,128)(2,1)S(1)} collective-permute-done((bf16[2,168,512]{2,1,0:T(8,128)(2,1)S(1)}, bf16[2,168,512]{2,1,0:T(8,128)(2,1)S(1)}, u32[]{:S(2)}, u32[]{:S(2)}) %collective-permute-start.26) | collective-permute-done | bytes 344096 | tf_op jit(solution)/shard_map/ppermute | solution.py:42
  152.9 7.9 %collective-permute-done.28.refs_9_ = bf16[2,168,512]{2,1,0:T(8,128)(2,1)S(1)} collective-permute-done((bf16[2,168,512]{2,1,0:T(8,128)(2,1)S(1)}, bf16[2,168,512]{2,1,0:T(8,128)(2,1)S(1)}, u32[]{:S(2)}, u32[]{:S(2)}) %collective-permute-start.28) | collective-permute-done | bytes 344096 | tf_op jit(solution)/shard_map/ppermute | solution.py:42
  162.2 3.9 %collective-permute-start.37 = (bf16[264,512]{1,0:T(8,128)(2,1)S(1)}, bf16[264,512]{1,0:T(8,128)(2,1)S(1)}, u32[]{:S(2)}, u32[]{:S(2)}) collective-permute-start(bf16[264,512]{1,0:T(8,128)(2,1)S(1)} %get-tuple-element.104), channel_id=1, source_target_pairs={{0,2},{1,3},{2,0},{3,1},{4,6},{5,7},{6,4},{7,5},{8,10},{9,11},{10,... | collective-permute-start | bytes 811016 | tf_op jit(solution)/shard_map/ppermute | solution.py:42
  170.7 4.8 %collective-permute-done.39.refs_5_ = bf16[256,512]{1,0:T(8,128)(2,1)S(1)} collective-permute-done((bf16[256,512]{1,0:T(8,128)(2,1)S(1)}, bf16[256,512]{1,0:T(8,128)(2,1)S(1)}, u32[]{:S(2)}, u32[]{:S(2)}) %collective-permute-start.39) | collective-permute-done | bytes 262176 | tf_op jit(solution)/shard_map/ppermute | solution.py:42
  176.0 3.4 %collective-permute-done.36.refs_1_ = bf16[264,512]{1,0:T(8,128)(2,1)S(1)} collective-permute-done((bf16[264,512]{1,0:T(8,128)(2,1)S(1)}, bf16[264,512]{1,0:T(8,128)(2,1)S(1)}, u32[]{:S(2)}, u32[]{:S(2)}) %collective-permute-start.36) | collective-permute-done | bytes 270368 | tf_op jit(solution)/shard_map/ppermute | solution.py:42
  179.7 3.5 %collective-permute-start.42 = (bf16[1,256,1024]{2,1,0:T(8,128)(2,1)S(1)}, bf16[1,256,1024]{2,1,0:T(8,128)(2,1)S(1)}, u32[]{:S(2)}, u32[]{:S(2)}) collective-permute-start(bf16[1,256,1024]{2,1,0:T(8,128)(2,1)S(1)} %finish.1), channel_id=1, source_target_pairs={{16,0},{32,16},{48,32},{64,48},{80,64},{96,80},{112,96},{17,1},{33... | collective-permute-start | bytes 1572872 | tf_op jit(solution)/shard_map/ppermute | solution.py:407
  183.4 6.5 %weight_grads.2 = (bf16[4,1024,384]{2,1,0:T(8,128)(2,1)}, bf16[4,1024,384]{2,1,0:T(8,128)(2,1)}) custom-call(s32[64]{0:T(128)S(1)} %reshape_squeeze.3.count_ref, bf16[4,640,1024]{2,1,0:T(8,128)(2,1)} %bitcast.58, bf16[4,640,384]{2,1,0:T(8,128)(2,1)} %bitcast.60, bf16[4,640,384]{2,1,0:T(8,128)(2,1)} %bitcast.62), custom_call_target="tpu_custom_call" | custom-call | tf_op jit(solution)/shard_map/weight_grads/pallas_call | solution.py:327
  189.9 6.4 %weight_grads.3 = (bf16[4,1024,384]{2,1,0:T(8,128)(2,1)}, bf16[4,1024,384]{2,1,0:T(8,128)(2,1)}) custom-call(s32[64]{0:T(128)S(1)} %reshape_squeeze.3.count_ref, bf16[4,640,1024]{2,1,0:T(8,128)(2,1)} %bitcast.59, bf16[4,640,384]{2,1,0:T(8,128)(2,1)} %bitcast.61, bf16[4,640,384]{2,1,0:T(8,128)(2,1)} %bitcast.63, ...), custom_call_target="tpu_custom_call", output_to_operand_aliasing={{0}: (4, {}), {1}: (5, {})} | custom-call | tf_op jit(solution)/shard_map/weight_grads/pallas_call | solution.py:327
  (98 shorter events, 68.2 us)
Async XLA Ops:
  3.8 26.3 %collective-permute-start.5 = (bf16[264,1024]{1,0:T(8,128)(2,1)}, bf16[264,1024]{1,0:T(8,128)(2,1)S(1)}, u32[]{:S(2)}, u32[]{:S(2)}) collective-permute-start(bf16[264,1024]{1,0:T(8,128)(2,1)} %get-tuple-element.114.refs_4_.refs_1_), channel_id=1, source_target_pairs={{0,12},{1,13},{2,14},{3,15},{4,0},{5,1},{6,2},{7,3},{8,4},{9,5},{1... | collective-permute-start | bytes 1622024 | tf_op jit(solution)/shard_map/ppermute | solution.py:42
  7.4 26.0 %collective-permute-start.4 = (bf16[264,1024]{1,0:T(8,128)(2,1)}, bf16[264,1024]{1,0:T(8,128)(2,1)}, u32[]{:S(2)}, u32[]{:S(2)}) collective-permute-start(bf16[264,1024]{1,0:T(8,128)(2,1)} %get-tuple-element.114.refs_4_.refs_1_), channel_id=1, source_target_pairs={{0,8},{1,9},{2,10},{3,11},{4,12},{5,13},{6,14},{7,15},{8,0},{9,1},... | collective-permute-start | bytes 1622024 | tf_op jit(solution)/shard_map/ppermute | solution.py:42
  7.7 27.3 %collective-permute-start.3 = (bf16[264,1024]{1,0:T(8,128)(2,1)}, bf16[264,1024]{1,0:T(8,128)(2,1)}, u32[]{:S(2)}, u32[]{:S(2)}) collective-permute-start(bf16[264,1024]{1,0:T(8,128)(2,1)} %get-tuple-element.114.refs_4_.refs_1_), channel_id=1, source_target_pairs={{0,4},{1,5},{2,6},{3,7},{4,8},{5,9},{6,10},{7,11},{8,12},{9,13},{1... | collective-permute-start | bytes 1622024 | tf_op jit(solution)/shard_map/ppermute | solution.py:42
  8.4 31.3 %collective-permute-start.2 = (bf16[264,1024]{1,0:T(8,128)(2,1)}, bf16[264,1024]{1,0:T(8,128)(2,1)}, u32[]{:S(2)}, u32[]{:S(2)}) collective-permute-start(bf16[264,1024]{1,0:T(8,128)(2,1)} %get-tuple-element.115.refs_0_.meta), channel_id=1, source_target_pairs={{0,3},{1,0},{2,1},{3,2},{4,7},{5,4},{6,5},{7,6},{8,11},{9,8},{10,9... | collective-permute-start | bytes 1622024 | tf_op jit(solution)/shard_map/ppermute | solution.py:42
  12.2 27.5 %collective-permute-start.1 = (bf16[264,1024]{1,0:T(8,128)(2,1)}, bf16[264,1024]{1,0:T(8,128)(2,1)}, u32[]{:S(2)}, u32[]{:S(2)}) collective-permute-start(bf16[264,1024]{1,0:T(8,128)(2,1)} %get-tuple-element.115.refs_0_.meta), channel_id=1, source_target_pairs={{0,2},{1,3},{2,0},{3,1},{4,6},{5,7},{6,4},{7,5},{8,10},{9,11},{10,... | collective-permute-start | bytes 1622024 | tf_op jit(solution)/shard_map/ppermute | solution.py:42
  35.0 17.7 %collective-permute-start.7 = (bf16[4,40,1024]{2,1,0:T(8,128)(2,1)S(1)}, bf16[4,40,1024]{2,1,0:T(8,128)(2,1)S(1)}, u32[]{:S(2)}, u32[]{:S(2)}) collective-permute-start(bf16[4,40,1024]{2,1,0:T(8,128)(2,1)S(1)} %get-tuple-element.64), channel_id=1, source_target_pairs={{0,8},{1,9},{2,10},{3,11},{4,12},{5,13},{6,14},{7,15},{8,0},{9,1},... | collective-permute-start | bytes 983048 | tf_op jit(solution)/shard_map/ppermute | solution.py:42
  48.0 19.4 %collective-permute-start.18 = (bf16[2,3,40,1024]{3,2,1,0:T(8,128)(2,1)S(1)}, bf16[2,3,40,1024]{3,2,1,0:T(8,128)(2,1)S(1)}, u32[]{:S(2)}, u32[]{:S(2)}) collective-permute-start(bf16[2,3,40,1024]{3,2,1,0:T(8,128)(2,1)S(1)} %get-tuple-element.80), channel_id=1, source_target_pairs={{0,4},{1,5},{2,6},{3,7},{4,8},{5,9},{6,10},{7,11},{8,12},{9,13},{1... | collective-permute-start | bytes 1474568 | tf_op jit(solution)/shard_map/ppermute | solution.py:42
  52.7 20.6 %collective-permute-start.19 = (bf16[2,3,40,1024]{3,2,1,0:T(8,128)(2,1)S(1)}, bf16[2,3,40,1024]{3,2,1,0:T(8,128)(2,1)S(1)}, u32[]{:S(2)}, u32[]{:S(2)}) collective-permute-start(bf16[2,3,40,1024]{3,2,1,0:T(8,128)(2,1)S(1)} %get-tuple-element.81), channel_id=1, source_target_pairs={{0,8},{1,9},{2,10},{3,11},{4,12},{5,13},{6,14},{7,15},{8,0},{9,1},... | collective-permute-start | bytes 1474568 | tf_op jit(solution)/shard_map/ppermute | solution.py:42
  56.5 19.6 %collective-permute-start.20 = (bf16[2,3,40,1024]{3,2,1,0:T(8,128)(2,1)S(1)}, bf16[2,3,40,1024]{3,2,1,0:T(8,128)(2,1)S(1)}, u32[]{:S(2)}, u32[]{:S(2)}) collective-permute-start(bf16[2,3,40,1024]{3,2,1,0:T(8,128)(2,1)S(1)} %get-tuple-element.82), channel_id=1, source_target_pairs={{0,12},{1,13},{2,14},{3,15},{4,0},{5,1},{6,2},{7,3},{8,4},{9,5},{1... | collective-permute-start | bytes 1474568 | tf_op jit(solution)/shard_map/ppermute | solution.py:42
  59.0 17.5 %collective-permute-start.21 = (bf16[2,3,40,1024]{3,2,1,0:T(8,128)(2,1)S(1)}, bf16[2,3,40,1024]{3,2,1,0:T(8,128)(2,1)S(1)}, u32[]{:S(2)}, u32[]{:S(2)}) collective-permute-start(bf16[2,3,40,1024]{3,2,1,0:T(8,128)(2,1)S(1)} %get-tuple-element.84), channel_id=1, source_target_pairs={{0,1},{1,2},{2,3},{3,0},{4,5},{5,6},{6,7},{7,4},{8,9},{9,10},{10,1... | collective-permute-start | bytes 1474568 | tf_op jit(solution)/shard_map/ppermute | solution.py:42
  67.5 17.8 %collective-permute-start.23 = (bf16[2,3,40,1024]{3,2,1,0:T(8,128)(2,1)S(1)}, bf16[2,3,40,1024]{3,2,1,0:T(8,128)(2,1)S(1)}, u32[]{:S(2)}, u32[]{:S(2)}) collective-permute-start(bf16[2,3,40,1024]{3,2,1,0:T(8,128)(2,1)S(1)} %get-tuple-element.86), channel_id=1, source_target_pairs={{0,3},{1,0},{2,1},{3,2},{4,7},{5,4},{6,5},{7,6},{8,11},{9,8},{10,9... | collective-permute-start | bytes 1474568 | tf_op jit(solution)/shard_map/ppermute | solution.py:42
  76.1 21.0 %collective-permute-start.10 = (bf16[2,3,40,1024]{3,2,1,0:T(8,128)(2,1)S(1)}, bf16[2,3,40,1024]{3,2,1,0:T(8,128)(2,1)S(1)}, u32[]{:S(2)}, u32[]{:S(2)}) collective-permute-start(bf16[2,3,40,1024]{3,2,1,0:T(8,128)(2,1)S(1)} %get-tuple-element.68), channel_id=1, source_target_pairs={{0,8},{1,9},{2,10},{3,11},{4,12},{5,13},{6,14},{7,15},{8,0},{9,1},... | collective-permute-start | bytes 1474568 | tf_op jit(solution)/shard_map/ppermute | solution.py:42
  76.5 21.4 %collective-permute-start.11 = (bf16[2,3,40,1024]{3,2,1,0:T(8,128)(2,1)S(1)}, bf16[2,3,40,1024]{3,2,1,0:T(8,128)(2,1)S(1)}, u32[]{:S(2)}, u32[]{:S(2)}) collective-permute-start(bf16[2,3,40,1024]{3,2,1,0:T(8,128)(2,1)S(1)} %get-tuple-element.69), channel_id=1, source_target_pairs={{0,12},{1,13},{2,14},{3,15},{4,0},{5,1},{6,2},{7,3},{8,4},{9,5},{1... | collective-permute-start | bytes 1474568 | tf_op jit(solution)/shard_map/ppermute | solution.py:42
  79.5 21.9 %collective-permute-start.15 = (bf16[2,3,40,1024]{3,2,1,0:T(8,128)(2,1)S(1)}, bf16[2,3,40,1024]{3,2,1,0:T(8,128)(2,1)S(1)}, u32[]{:S(2)}, u32[]{:S(2)}) collective-permute-start(bf16[2,3,40,1024]{3,2,1,0:T(8,128)(2,1)S(1)} %get-tuple-element.75), channel_id=1, source_target_pairs={{0,1},{1,2},{2,3},{3,0},{4,5},{5,6},{6,7},{7,4},{8,9},{9,10},{10,1... | collective-permute-start | bytes 1474568 | tf_op jit(solution)/shard_map/ppermute | solution.py:42
  85.3 20.1 %collective-permute-start.16 = (bf16[2,3,40,1024]{3,2,1,0:T(8,128)(2,1)S(1)}, bf16[2,3,40,1024]{3,2,1,0:T(8,128)(2,1)S(1)}, u32[]{:S(2)}, u32[]{:S(2)}) collective-permute-start(bf16[2,3,40,1024]{3,2,1,0:T(8,128)(2,1)S(1)} %get-tuple-element.76), channel_id=1, source_target_pairs={{0,2},{1,3},{2,0},{3,1},{4,6},{5,7},{6,4},{7,5},{8,10},{9,11},{10,... | collective-permute-start | bytes 1474568 | tf_op jit(solution)/shard_map/ppermute | solution.py:42
  86.6 19.9 %collective-permute-start.17 = (bf16[2,3,40,1024]{3,2,1,0:T(8,128)(2,1)S(1)}, bf16[2,3,40,1024]{3,2,1,0:T(8,128)(2,1)S(1)}, u32[]{:S(2)}, u32[]{:S(2)}) collective-permute-start(bf16[2,3,40,1024]{3,2,1,0:T(8,128)(2,1)S(1)} %get-tuple-element.77), channel_id=1, source_target_pairs={{0,3},{1,0},{2,1},{3,2},{4,7},{5,4},{6,5},{7,6},{8,11},{9,8},{10,9... | collective-permute-start | bytes 1474568 | tf_op jit(solution)/shard_map/ppermute | solution.py:42
  97.1 20.6 %collective-permute-start.31 = (bf16[2,4,40,512]{3,2,1,0:T(8,128)(2,1)S(1)}, bf16[2,4,40,512]{3,2,1,0:T(8,128)(2,1)S(1)}, u32[]{:S(2)}, u32[]{:S(2)}) collective-permute-start(bf16[2,4,40,512]{3,2,1,0:T(8,128)(2,1)S(1)} %get-tuple-element.97), channel_id=1, source_target_pairs={{0,3},{1,0},{2,1},{3,2},{4,7},{5,4},{6,5},{7,6},{8,11},{9,8},{10,9... | collective-permute-start | bytes 983048 | tf_op jit(solution)/shard_map/ppermute | solution.py:42
  97.9 19.8 %collective-permute-start.33 = (bf16[2,4,40,512]{3,2,1,0:T(8,128)(2,1)S(1)}, bf16[2,4,40,512]{3,2,1,0:T(8,128)(2,1)S(1)}, u32[]{:S(2)}, u32[]{:S(2)}) collective-permute-start(bf16[2,4,40,512]{3,2,1,0:T(8,128)(2,1)S(1)} %get-tuple-element.99), channel_id=1, source_target_pairs={{0,2},{1,3},{2,0},{3,1},{4,6},{5,7},{6,4},{7,5},{8,10},{9,11},{10,... | collective-permute-start | bytes 983048 | tf_op jit(solution)/shard_map/ppermute | solution.py:42
  101.4 38.9 %collective-permute-start.25 = (bf16[2,168,512]{2,1,0:T(8,128)(2,1)S(1)}, bf16[2,168,512]{2,1,0:T(8,128)(2,1)S(1)}, u32[]{:S(2)}, u32[]{:S(2)}) collective-permute-start(bf16[2,168,512]{2,1,0:T(8,128)(2,1)S(1)} %get-tuple-element.89), channel_id=1, source_target_pairs={{0,12},{1,13},{2,14},{3,15},{4,0},{5,1},{6,2},{7,3},{8,4},{9,5},{1... | collective-permute-start | bytes 1032200 | tf_op jit(solution)/shard_map/ppermute | solution.py:42
  117.7 20.6 %collective-permute-start.34 = (bf16[2,4,40,512]{3,2,1,0:T(8,128)(2,1)S(1)}, bf16[2,4,40,512]{3,2,1,0:T(8,128)(2,1)S(1)}, u32[]{:S(2)}, u32[]{:S(2)}) collective-permute-start(bf16[2,4,40,512]{3,2,1,0:T(8,128)(2,1)S(1)} %get-tuple-element.100), channel_id=1, source_target_pairs={{0,1},{1,2},{2,3},{3,0},{4,5},{5,6},{6,7},{7,4},{8,9},{9,10},{10,1... | collective-permute-start | bytes 983048 | tf_op jit(solution)/shard_map/ppermute | solution.py:42
  121.5 27.7 %collective-permute-start.27 = (bf16[2,168,512]{2,1,0:T(8,128)(2,1)S(1)}, bf16[2,168,512]{2,1,0:T(8,128)(2,1)S(1)}, u32[]{:S(2)}, u32[]{:S(2)}) collective-permute-start(bf16[2,168,512]{2,1,0:T(8,128)(2,1)S(1)} %get-tuple-element.91), channel_id=1, source_target_pairs={{0,8},{1,9},{2,10},{3,11},{4,12},{5,13},{6,14},{7,15},{8,0},{9,1},... | collective-permute-start | bytes 1032200 | tf_op jit(solution)/shard_map/ppermute | solution.py:42
  127.5 21.7 %collective-permute-start.29 = (bf16[2,168,512]{2,1,0:T(8,128)(2,1)S(1)}, bf16[2,168,512]{2,1,0:T(8,128)(2,1)S(1)}, u32[]{:S(2)}, u32[]{:S(2)}) collective-permute-start(bf16[2,168,512]{2,1,0:T(8,128)(2,1)S(1)} %get-tuple-element.93), channel_id=1, source_target_pairs={{0,4},{1,5},{2,6},{3,7},{4,8},{5,9},{6,10},{7,11},{8,12},{9,13},{1... | collective-permute-start | bytes 1032200 | tf_op jit(solution)/shard_map/ppermute | solution.py:42
  140.3 20.5 %collective-permute-start.28 = (bf16[2,168,512]{2,1,0:T(8,128)(2,1)S(1)}, bf16[2,168,512]{2,1,0:T(8,128)(2,1)S(1)}, u32[]{:S(2)}, u32[]{:S(2)}) collective-permute-start(bf16[2,168,512]{2,1,0:T(8,128)(2,1)S(1)} %get-tuple-element.92), channel_id=1, source_target_pairs={{0,4},{1,5},{2,6},{3,7},{4,8},{5,9},{6,10},{7,11},{8,12},{9,13},{1... | collective-permute-start | bytes 1032200 | tf_op jit(solution)/shard_map/ppermute | solution.py:42
  179.7 18.4 %collective-permute-start.42 = (bf16[1,256,1024]{2,1,0:T(8,128)(2,1)S(1)}, bf16[1,256,1024]{2,1,0:T(8,128)(2,1)S(1)}, u32[]{:S(2)}, u32[]{:S(2)}) collective-permute-start(bf16[1,256,1024]{2,1,0:T(8,128)(2,1)S(1)} %finish.1), channel_id=1, source_target_pairs={{16,0},{32,16},{48,32},{64,48},{80,64},{96,80},{112,96},{17,1},{33... | collective-permute-start | bytes 1572872 | tf_op jit(solution)/shard_map/ppermute | solution.py:407
  (26 other events, 450.8 us)
